TPU v7x, 32 devices: a 4x4x1 block of a 4x4x8 slice. The times are simulated.
32 devices in a mesh: dp: 1 (over z), tp: 4 (over y), sp: 8 (over x, core).
Axes of the slice: x: 4, y: 4, z: 1, core: 2. Of those that a mesh axis runs over, the one named last changes fastest.
The devices are a block of a 4x4x8 slice.
Arguments:
- tokens: bfloat16 [64, 3840], P('dp')
- positions: int32 [64], P('dp')
- cache_k: bfloat16 [64, 1024, 8, 256], P('dp', 'sp', 'tp')
- cache_v: bfloat16 [64, 1024, 8, 256], P('dp', 'sp', 'tp')
- attn_gain: bfloat16 [3840], replicated
- w_q: bfloat16 [3840, 4096], P(None, 'tp')
- w_k: bfloat16 [3840, 2048], P(None, 'tp')
- w_v: bfloat16 [3840, 2048], P(None, 'tp')
- w_o: bfloat16 [4096, 3840], P('tp')
- mlp_gain: bfloat16 [3840], replicated
- w_gate: bfloat16 [3840, 15360], P(None, 'tp')
- w_up: bfloat16 [3840, 15360], P(None, 'tp')
- w_down: bfloat16 [15360, 3840], P('tp')
Outputs:
- output 1: bfloat16 [64, 3840], P('dp')
- output 2: bfloat16 [64, 1024, 8, 256], P('dp', 'sp', 'tp')
- output 3: bfloat16 [64, 1024, 8, 256], P('dp', 'sp', 'tp')
All inputs are finite; a program needn't handle non-finite values.
Results may differ from a plain program's by a relative error of at most 0.00836772.
Values sent between devices are 32-bit elements.
A program may use at most 768 MiB of HBM per device.

v0:
```python
import math
import jax
import jax.numpy as jnp
from jax import lax
from jax.sharding import PartitionSpec as P

NORM_EPS = 1e-5
ROPE_THETA = 10000.0


def rms_norm(values, gain):
    wide = values.astype(jnp.float32)
    inv_rms = lax.rsqrt(jnp.mean(wide * wide, axis=-1, keepdims=True) + NORM_EPS)
    return (wide * inv_rms * gain.astype(jnp.float32)).astype(jnp.bfloat16)


def rope_tables(positions, head_dim):
    frequencies = ROPE_THETA ** (-2.0 * jnp.arange(head_dim // 2, dtype=jnp.float32) / head_dim)
    angles = positions.astype(jnp.float32)[:, None] * frequencies[None, :]
    return jnp.cos(angles)[:, None, :], jnp.sin(angles)[:, None, :]


def apply_rope(vectors, cos_table, sin_table):
    half = vectors.shape[-1] // 2
    first = vectors[..., :half]
    second = vectors[..., half:]
    return jnp.concatenate([first * cos_table - second * sin_table, second * cos_table + first * sin_table], axis=-1)


def solution(mesh):
    sp_size = mesh.shape["sp"]
    cache_spec = P("dp", "sp", "tp", None)
    row_spec = P("dp", None)
    col_spec = P(None, "tp")
    in_specs = (row_spec, P("dp"), cache_spec, cache_spec, P(None), col_spec, col_spec, col_spec, P("tp", None), P(None), col_spec, col_spec, P("tp", None))
    out_specs = (row_spec, cache_spec, cache_spec)

    def local_step(tokens, positions, cache_k, cache_v, attn_gain, w_q, w_k, w_v, w_o, mlp_gain, w_gate, w_up, w_down):
        rows = tokens.shape[0]
        local_slots = cache_k.shape[1]
        kv_local = cache_k.shape[2]
        head_dim = cache_k.shape[3]
        heads_local = w_q.shape[1] // head_dim
        group = heads_local // kv_local
        slots = local_slots * sp_size
        slot_ids = lax.axis_index("sp") * local_slots + jnp.arange(local_slots)

        normed = rms_norm(tokens, attn_gain)
        cos_table, sin_table = rope_tables(positions, head_dim)
        q_lin = jnp.dot(normed, w_q, preferred_element_type=jnp.float32).reshape(rows, heads_local, head_dim)
        k_lin = jnp.dot(normed, w_k, preferred_element_type=jnp.float32).reshape(rows, kv_local, head_dim)
        v_new = jnp.dot(normed, w_v, preferred_element_type=jnp.float32).astype(jnp.bfloat16).reshape(rows, kv_local, head_dim)
        q_rot = apply_rope(q_lin, cos_table, sin_table).astype(jnp.bfloat16).reshape(rows, kv_local, group, head_dim)
        k_rot = apply_rope(k_lin, cos_table, sin_table).astype(jnp.bfloat16)

        hit_mask = (slot_ids[None, :] == (positions % slots)[:, None])[:, :, None, None]
        new_k = jnp.where(hit_mask, k_rot[:, None], cache_k)
        new_v = jnp.where(hit_mask, v_new[:, None], cache_v)

        scores = jnp.einsum("bkgd,bskd->bkgs", q_rot, new_k, preferred_element_type=jnp.float32) * (1.0 / math.sqrt(head_dim))
        valid = ((positions[:, None] >= slots - 1) | (slot_ids[None, :] <= positions[:, None]))[:, None, None, :]
        local_max = jnp.max(jnp.where(valid, scores, -jnp.inf), axis=-1)
        exp_scores = jnp.exp(jnp.where(valid, scores - local_max[..., None], -jnp.inf))
        local_sum = jnp.sum(exp_scores, axis=-1)
        local_out = jnp.einsum("bkgs,bskd->bkgd", exp_scores.astype(jnp.bfloat16), new_v, preferred_element_type=jnp.float32)

        global_max = lax.pmax(local_max, "sp")
        factor = jnp.exp(local_max - global_max)
        packed = jnp.concatenate([local_out * factor[..., None], (local_sum * factor)[..., None]], axis=-1)
        total = lax.psum(packed, "sp")
        attended = (total[..., :head_dim] / total[..., head_dim:]).astype(jnp.bfloat16).reshape(rows, heads_local * head_dim)

        attn_proj = lax.psum(jnp.dot(attended, w_o, preferred_element_type=jnp.float32), "tp")
        hidden = (tokens.astype(jnp.float32) + attn_proj).astype(jnp.bfloat16)
        normed_mlp = rms_norm(hidden, mlp_gain)
        gate_proj = jnp.dot(normed_mlp, w_gate, preferred_element_type=jnp.float32)
        up_proj = jnp.dot(normed_mlp, w_up, preferred_element_type=jnp.float32)
        activated = (jax.nn.silu(gate_proj) * up_proj).astype(jnp.bfloat16)
        mlp_down = lax.psum(jnp.dot(activated, w_down, preferred_element_type=jnp.float32), "tp")
        layer_out = (hidden.astype(jnp.float32) + mlp_down).astype(jnp.bfloat16)
        return layer_out, new_k, new_v

    return jax.shard_map(local_step, mesh=mesh, in_specs=in_specs, out_specs=out_specs, check_vma=False)
```

profile of v0, /device:TPU:97, one launch (start us, length us, event | category | flops | bytes accessed | tf_op | source)
XLA Modules:
  0.0 272.9 jit_solution(2882561146930211774)
XLA Ops:
  7.2 0.0 copy-start
  7.2 0.1 all-reduce.4.cloned.1.call-start
  7.3 0.7 broadcast_compare_fusion.1
  8.0 0.7 fusion.46
  8.7 1.2 fusion.12
  10.0 0.7 convert_element_type.49
  10.7 3.1 %convolution_convert_fusion = bf16[64,512]{1,0:T(8,128)(2,1)S(1)} fusion(bf16[3840,512]{1,0:T(8,128)(2,1)} %param.20, bf16[64,3840]{1,0:T(8,128)(2,1)} %param.13, f32[3840]{0:T(1024)S(1)} %convert_element_type.49, f32[64]{0:T(128)S(1)} %add_rsqrt_fusion.1), kind=kOutput, calls=%fused_computation.15 | convolution fusion | flops 252674048 | bytes 4504832 | tf_op jit(solution)/shard_map/dot_general | solution.py:52
  13.8 0.0 copy-start.3
  13.8 3.1 %fusion.41 = f32[64,512]{1,0:T(8,128)S(1)} fusion(bf16[3840,512]{1,0:T(8,128)(2,1)} %param.19, bf16[64,3840]{1,0:T(8,128)(2,1)} %param.13, f32[3840]{0:T(1024)S(1)} %convert_element_type.49, f32[64]{0:T(128)S(1)} %add_rsqrt_fusion.1), kind=kOutput, calls=%fused_computation.66 | convolution fusion | flops 252641280 | bytes 4570368 | tf_op jit(solution)/shard_map/dot_general | solution.py:51
  17.0 0.1 reshape.175
  17.1 0.0 copy-done
  17.1 4.8 %fusion.43 = f32[64,1024]{1,0:T(8,128)S(1)} fusion(bf16[3840,1024]{1,0:T(8,128)(2,1)} %param.18, bf16[64,3840]{1,0:T(8,128)(2,1)S(1)} %copy-done, f32[3840]{0:T(1024)S(1)} %convert_element_type.49, f32[64]{0:T(128)S(1)} %add_rsqrt_fusion.1), kind=kOutput, calls=%fused_computation.67 | convolution fusion | flops 504299520 | bytes 8633600 | tf_op jit(solution)/shard_map/dot_general | solution.py:50
  21.8 0.1 reshape.174
  22.0 0.2 multiply_cosine_fusion
  22.2 0.1 subtract_convert_fusion.1
  22.3 0.1 subtract_convert_fusion
  22.3 0.1 pad_maximum_fusion.1
  22.4 0.0 copy-done.3
  22.4 0.1 compare_or_fusion
  22.5 21.5 %broadcast_select_fusion = (bf16[64,128,2,256]{3,2,1,0:T(2,128)(2,1)}, bf16[64,128,2,256]{3,2,1,0:T(2,128)(2,1)S(1)}) fusion(bf16[64,128,2,256]{3,2,1,0:T(2,128)(2,1)} %param.16, pred[64,128]{1,0:T(8,128)(4,1)S(1)} %get-tuple-element.16, bf16[64,2,256]{2,1,0:T(2,128)(2,1)S(1)} %broadcast_in_dim.67, bf16[64,128,2,256]{3,2,1,0:T(2,128)(2,1)} %param.15, ...), kind=kLoop, calls=%fused_computation | loop fusion | flops 8388608 | bytes 33693696 | tf_op jit(solution)/shard_map/jit(_where)/select_n | solution.py:58
  44.0 0.0 copy-start.1
  44.0 3.4 %copy-done.1 = bf16[64,128,2,256]{3,2,1,0:T(2,128)(2,1)} copy-done((bf16[64,128,2,256]{3,2,1,0:T(2,128)(2,1)}, bf16[64,128,2,256]{3,2,1,0:T(2,128)(2,1)S(1)}, u32[]{:S(2)}) %copy-start.1) | copy-done | bytes 8388632
  47.4 2.4 select_reduce_fusion
  49.8 24.5 %pmax.7 = f32[64,2,2]{2,1,0:T(2,128)S(1)} all-reduce(f32[64,2,2]{2,1,0:T(2,128)S(1)} %get-tuple-element.19), channel_id=1, replica_groups=mesh['dp'=1,'tp'=4,'sp'=8] {'sp'}, use_global_device_ids=true, to_apply=%region_2.3 | all-reduce | flops 256 | bytes 2048 | tf_op jit(solution)/shard_map/pmax | solution.py:67
  74.3 0.4 fusion.35
  74.7 0.1 multiply_bitcast_fusion
  74.8 0.9 copy.28
  75.7 4.6 %fusion.6 = f32[64,2,2,256]{3,2,1,0:T(2,128)S(1)} fusion(bf16[64,128,2,256]{3,2,1,0:T(2,128)(2,1)} %get-tuple-element.11, f32[64,2,2]{2,1,0:T(2,128)S(1)} %get-tuple-element.6, f32[64,2,2,128]{3,2,1,0:T(2,128)S(1)} %get-tuple-element.20, pred[64,128]{1,0:T(8,128)(4,1)S(1)} %get-tuple-element.15, f32[64,2,2]{2,1,0:T(2,128)S(1)} %get-tuple-element.19), kind=kOutput, calls=%fused_computation.16 | convolution fusion | flops 16941056 | bytes 8792064 | tf_op jit(solution)/shard_map/bkgs,bskd->bkgd/dot_general | solution.py:65
  80.3 0.9 pad_maximum_fusion
  81.3 0.1 all-reduce.4.cloned.1.call-update
  81.3 0.1 all-reduce.6.cloned.1.call-start
  81.4 56.7 %all-reduce.4.cloned.1.call-done = f32[64,2,2,257]{3,2,1,0:T(2,128)} async-done(((f32[64,2,2,257]{3,2,1,0:T(2,128)}), f32[64,2,2,257]{3,2,1,0:T(2,128)}) %all-reduce.4.cloned.1.call-update) | async-done | bytes 263184 | tf_op jit(solution)/shard_map/psum | solution.py:70
  138.1 0.9 slice.29
  139.0 0.9 copy.33
  139.9 0.0 copy-start.2
  139.9 1.2 fusion.26
  141.1 0.1 reshape.176
  141.1 5.7 %fusion.47 = f32[64,3840]{1,0:T(8,128)} fusion(bf16[64,1024]{1,0:T(8,128)(2,1)S(1)} %reshape.176, bf16[1024,3840]{1,0:T(8,128)(2,1)} %param.21), kind=kOutput, calls=%fused_computation.69 | convolution fusion | flops 503316480 | bytes 8978432 | tf_op jit(solution)/shard_map/dot_general | solution.py:73
  146.9 0.1 all-reduce.6.cloned.1.call-update
  146.9 0.2 all-reduce.8.cloned.1.call-start
  147.2 0.0 copy-done.2
  147.2 39.4 %all-reduce.6.cloned.1.call-done = f32[64,3840]{1,0:T(8,128)} async-done(((f32[64,3840]{1,0:T(8,128)}), f32[64,3840]{1,0:T(8,128)}) %all-reduce.6.cloned.1.call-update) | async-done | bytes 983056 | tf_op jit(solution)/shard_map/psum | solution.py:73
  186.5 1.4 fusion.16
  188.0 12.1 %fusion.29 = f32[64,3840]{1,0:T(8,128)S(1)} fusion(bf16[3840,3840]{1,0:T(8,128)(2,1)} %param.23, bf16[64,3840]{1,0:T(8,128)(2,1)S(1)} %get-tuple-element.4, f32[3840]{0:T(1024)S(1)} %convert_element_type.57, f32[64]{0:T(128)S(1)} %add_rsqrt_fusion), kind=kOutput, calls=%fused_computation.35 | convolution fusion | flops 1888419840 | bytes 30981376 | tf_op jit(solution)/shard_map/dot_general | solution.py:76
  200.1 22.7 %fusion.5 = f32[64,3840]{1,0:T(8,128)} fusion(bf16[3840,3840]{1,0:T(8,128)(2,1)} %param.25, bf16[3840,3840]{1,0:T(8,128)(2,1)} %param.24, f32[64,3840]{1,0:T(8,128)S(1)} %fusion.29, bf16[64,3840]{1,0:T(8,128)(2,1)S(1)} %get-tuple-element.4, f32[3840]{0:T(1024)S(1)} %convert_element_type.57, f32[64]{0:T(128)S(1)} %add_rsqrt_fusion), kind=kOutput, calls=%fused_computation.8 | convolution fusion | flops 3777331200 | bytes 61455616 | tf_op jit(solution)/shard_map/dot_general | solution.py:79
  222.9 0.1 all-reduce.8.cloned.1.call-update
  222.9 41.4 %all-reduce.8.cloned.1.call-done = f32[64,3840]{1,0:T(8,128)} async-done(((f32[64,3840]{1,0:T(8,128)}), f32[64,3840]{1,0:T(8,128)}) %all-reduce.8.cloned.1.call-update) | async-done | bytes 983056 | tf_op jit(solution)/shard_map/psum | solution.py:79
  264.3 2.1 fusion.19
  (6 shorter events, 0.1 us)
Async XLA Ops:
  7.2 9.9 %copy-start = (bf16[64,3840]{1,0:T(8,128)(2,1)S(1)}, bf16[64,3840]{1,0:T(8,128)(2,1)}, u32[]{:S(2)}) copy-start(bf16[64,3840]{1,0:T(8,128)(2,1)} %param.13) | copy-start | bytes 1474564
  7.2 130.9 %all-reduce.4.cloned.1.call-start = ((), (), s32[]{:S(2)}) async-start(), calls=%async_computation | async-start | bytes 786432 | tf_op jit(solution)/shard_map/psum | solution.py:70
  13.8 8.6 %copy-start.3 = (s32[64]{0:T(128)S(1)}, s32[64]{0:T(128)}, u32[]{:S(2)}) copy-start(s32[64]{0:T(128)} %param.14) | copy-start | bytes 772
  44.0 3.4 %copy-start.1 = (bf16[64,128,2,256]{3,2,1,0:T(2,128)(2,1)}, bf16[64,128,2,256]{3,2,1,0:T(2,128)(2,1)S(1)}, u32[]{:S(2)}) copy-start(bf16[64,128,2,256]{3,2,1,0:T(2,128)(2,1)S(1)} %get-tuple-element.12) | copy-start | bytes 25165828
  81.3 105.2 %all-reduce.6.cloned.1.call-start = ((), (), s32[]{:S(2)}) async-start(), calls=%async_computation.1 | async-start | bytes 1966080 | tf_op jit(solution)/shard_map/psum | solution.py:73
  139.9 7.3 %copy-start.2 = (bf16[3840]{0:T(1024)(128)(2,1)S(1)}, bf16[3840]{0:T(1024)(128)(2,1)}, u32[]{:S(2)}) copy-start(bf16[3840]{0:T(1024)(128)(2,1)} %param.22) | copy-start | bytes 23044
  146.9 117.4 %all-reduce.8.cloned.1.call-start = ((), (), s32[]{:S(2)}) async-start(), calls=%async_computation.2 | async-start | bytes 1966080 | tf_op jit(solution)/shard_map/psum | solution.py:79
Sparse Core Ops, SparseCore 0:
  81.4 56.5 all-reduce.3
  147.0 39.4 all-reduce.5
  223.0 41.2 all-reduce.7
where the time goes:
time: 275 us; the launch traced here: 273 us
  waiting for transfers between devices  138 us (50%)
  matrix products  58.6 us (21%)
  other arithmetic  31.5 us (11%)
  blocking collectives  24.5 us (9%)
  between operations  14 us (5%)
  local copies, waits for them, and re-layouts  6.41 us (2%)
    psum x1, waiting for transfers between devices, local_step(): total = lax.psum(packed, 'sp')  56.7 us
    psum x1, waiting for transfers between devices, local_step(): lax.psum(jnp.dot(activated, w_down, preferred_element_type=jnp.float32),...  41.4 us
    psum x1, waiting for transfers between devices, local_step(): lax.psum(jnp.dot(attended, w_o, preferred_element_type=jnp.float32), 'tp')  39.4 us
    pmax x1, blocking collectives, local_step(): global_max = lax.pmax(local_max, 'sp')  24.5 us
    dot_general x1, matrix products, local_step(): jnp.dot(activated, w_down, preferred_element_type=jnp.float32)  22.7 us
    select_n x1, other arithmetic, local_step(): new_v = jnp.where(hit_mask, v_new[:, None], cache_v)  21.5 us
    dot_general x1, matrix products, local_step(): gate_proj = jnp.dot(normed_mlp, w_gate, preferred_element_type=jnp.float32)  12.1 us
    dot_general x1, matrix products, local_step(): jnp.dot(attended, w_o, preferred_element_type=jnp.float32)  5.71 us
  transfers between devices with their start and end apart: 3, of which 3 were waited for; matrix products, arithmetic and copies ran while one was open for 0% of the time, Pallas kernels for 0%

commit v1 on v0

v1 whole, which is shorter than its diff:
```python
import functools, math
import jax, jax.numpy as jnp, numpy as np
from jax import lax
from jax.experimental import pallas as pl
from jax.experimental.pallas import tpu as pltpu

NORM_EPS = 1e-5
ROPE_THETA = 10000.0
GRP = 8
KSTEP = 768


def attend_kernel(sp_size, tok_ref, pos_ref, posv_ref, freq_ref, gain_ref, wq_hbm, wk_hbm, wv_hbm, ck_hbm, cv_hbm,
                  part_ref, nk_hbm, nv_hbm,
                  wq, wk, wv, kbuf, vbuf, acc, normed, qrows, knew, vnew, wsem, csem, osem):
    rows, width = tok_ref.shape
    slots_local = kbuf.shape[1]
    kv_heads = kbuf.shape[2]
    head = kbuf.shape[3]
    q_cols, k_cols = wq.shape[1], wk.shape[1]
    heads = q_cols // head
    half = head // 2
    slots = slots_local * sp_size
    my_first = lax.axis_index("sp") * slots_local
    groups = rows // GRP
    ksteps = width // KSTEP

    def wcopies(c):
        sl = pl.ds(pl.multiple_of(c * KSTEP, KSTEP), KSTEP)
        return [pltpu.make_async_copy(src.at[sl], dst.at[sl], wsem.at[i, c])
                for i, (src, dst) in enumerate(((wq_hbm, wq), (wk_hbm, wk), (wv_hbm, wv)))]

    def ccopies(g):
        sl = pl.ds(g * GRP, GRP)
        return [pltpu.make_async_copy(ck_hbm.at[sl], kbuf.at[sl], csem.at[0, g]),
                pltpu.make_async_copy(cv_hbm.at[sl], vbuf.at[sl], csem.at[1, g])]

    def ocopies(g):
        sl = pl.ds(g * GRP, GRP)
        return [pltpu.make_async_copy(kbuf.at[sl], nk_hbm.at[sl], osem.at[0, g]),
                pltpu.make_async_copy(vbuf.at[sl], nv_hbm.at[sl], osem.at[1, g])]

    for c in range(ksteps):
        for cp in wcopies(c):
            cp.start()
    for g in range(groups):
        for cp in ccopies(g):
            cp.start()

    wide = tok_ref[...].astype(jnp.float32)
    inv = lax.rsqrt(jnp.mean(wide * wide, axis=-1, keepdims=True) + NORM_EPS)
    normed[...] = (wide * inv * gain_ref[...].astype(jnp.float32)).astype(jnp.bfloat16)
    angles = posv_ref[...].astype(jnp.float32) * freq_ref[...]
    cos, sin = jnp.cos(angles), jnp.sin(angles)
    acc[...] = jnp.zeros_like(acc)

    @pl.loop(0, ksteps)
    def _(c):
        for cp in wcopies(c):
            cp.wait()
        sl = pl.ds(pl.multiple_of(c * KSTEP, KSTEP), KSTEP)
        lhs = normed[:, sl]
        for w, off, cols in ((wq, 0, q_cols), (wk, q_cols, k_cols), (wv, q_cols + k_cols, k_cols)):
            acc[:, off:off + cols] += jnp.dot(lhs, w[sl, :], preferred_element_type=jnp.float32)

    def rope(off):
        a = acc[:, off:off + half]
        b = acc[:, off + half:off + head]
        return jnp.concatenate([a * cos - b * sin, b * cos + a * sin], axis=-1)

    for h in range(heads):
        q = rope(h * head).astype(jnp.bfloat16).astype(jnp.float32)
        qrows[0, pl.ds(h, rows, stride=heads), :] = q[:, :half]
        qrows[1, pl.ds(h, rows, stride=heads), :] = q[:, half:]
    for h in range(kv_heads):
        knew[:, h, :] = rope(q_cols + h * head)
        off = q_cols + k_cols + h * head
        vnew[:, h, :] = acc[:, off:off + head]

    pair = 8 // heads
    merged = slots_local * kv_heads
    lane = lax.broadcasted_iota(jnp.int32, (8, merged), 1)
    row = lax.broadcasted_iota(jnp.int32, (8, merged), 0)
    lane_slot = my_first + lane // kv_heads
    same_head = (lane % kv_heads) == ((row % heads) // (heads // kv_heads))
    scale = 1.0 / math.sqrt(head)
    stat_lane = lax.broadcasted_iota(jnp.int32, (8, 128), 1)
    n_pairs = GRP // pair
    span = 128 // (2 * n_pairs)

    @pl.loop(0, groups)
    def _(g):
        for cp in ccopies(g):
            cp.wait()
        for i in range(GRP):
            b = g * GRP + i
            local = pos_ref[b] % slots - my_first

            @pl.when((local >= 0) & (local < slots_local))
            def _():
                kbuf[b, local] = knew[b].astype(jnp.bfloat16)
                vbuf[b, local] = vnew[b].astype(jnp.bfloat16)
        for cp in ocopies(g):
            cp.start()
        stat = jnp.zeros((8, 128), jnp.float32)
        for j in range(n_pairs):
            b0 = g * GRP + j * pair
            q_at = pl.ds(pl.multiple_of(b0 * heads, 8), 8)
            q8 = jnp.concatenate([qrows[0, q_at, :], qrows[1, q_at, :]], axis=-1).astype(jnp.bfloat16)
            s = None
            lim = None
            for i in range(pair):
                kk = kbuf[b0 + i].reshape(merged, head)
                si = lax.dot_general(q8, kk, (((1,), (1,)), ((), ())), preferred_element_type=jnp.float32)
                li = jnp.minimum(pos_ref[b0 + i], slots - 1)
                s = si if s is None else jnp.where(row < i * heads, s, si)
                lim = jnp.full((8, merged), li, jnp.int32) if lim is None else jnp.where(row < i * heads, lim, li)
            valid = same_head & (lane_slot <= lim)
            s = jnp.where(valid, s * scale, -jnp.inf)
            top = jnp.max(s, axis=-1, keepdims=True)
            safe = jnp.where(top == -jnp.inf, 0.0, top)
            p = jnp.exp(s - safe)
            total = jnp.sum(p, axis=-1, keepdims=True)
            out = None
            for i in range(pair):
                vv = vbuf[b0 + i].reshape(merged, head)
                mine = (row >= i * heads) & (row < (i + 1) * heads)
                oi = jnp.dot(jnp.where(mine, p, 0.0).astype(jnp.bfloat16), vv, preferred_element_type=jnp.float32)
                out = oi if out is None else out + oi
            part_ref[g, j * 8:(j + 1) * 8, :] = out
            lo = 2 * j * span
            stat = jnp.where((stat_lane >= lo) & (stat_lane < lo + span), top, stat)
            stat = jnp.where((stat_lane >= lo + span) & (stat_lane < lo + 2 * span), total, stat)
        part_ref[g, n_pairs * 8:, :128] = stat
        part_ref[g, n_pairs * 8:, 128:] = stat

    for g in range(groups):
        for cp in ocopies(g):
            cp.wait()


def attend(sp_size, tokens, positions, cache_k, cache_v, gain, w_q, w_k, w_v):
    rows, width = tokens.shape
    _, slots_local, kv_heads, head = cache_k.shape
    heads = w_q.shape[1] // head
    freq = jnp.asarray((np.float32(ROPE_THETA) ** (np.float32(-2.0) * np.arange(head // 2, dtype=np.float32) / np.float32(head))).astype(np.float32))[None, :]
    groups = rows // GRP
    chunk_rows = GRP * heads + 8
    any_spec = pl.BlockSpec(memory_space=pl.ANY)
    vm = pl.BlockSpec(memory_space=pltpu.VMEM)
    qkv_cols = w_q.shape[1] + 2 * w_k.shape[1]
    bf = jnp.bfloat16
    return pl.pallas_call(
        functools.partial(attend_kernel, sp_size),
        out_shape=(jax.ShapeDtypeStruct((groups, chunk_rows, head), jnp.float32),
                   jax.ShapeDtypeStruct(cache_k.shape, bf), jax.ShapeDtypeStruct(cache_v.shape, bf)),
        in_specs=[vm, pl.BlockSpec(memory_space=pltpu.SMEM), vm, vm, vm] + [any_spec] * 5,
        out_specs=(vm, any_spec, any_spec),
        scratch_shapes=[
            pltpu.VMEM(w_q.shape, bf), pltpu.VMEM(w_k.shape, bf), pltpu.VMEM(w_v.shape, bf),
            pltpu.VMEM(cache_k.shape, bf), pltpu.VMEM(cache_v.shape, bf),
            pltpu.VMEM((rows, qkv_cols), jnp.float32), pltpu.VMEM((rows, width), bf),
            pltpu.VMEM((2, rows * heads, head // 2), jnp.float32),
            pltpu.VMEM((rows, kv_heads, head), jnp.float32), pltpu.VMEM((rows, kv_heads, head), jnp.float32),
            pltpu.SemaphoreType.DMA((3, width // KSTEP)), pltpu.SemaphoreType.DMA((2, groups)), pltpu.SemaphoreType.DMA((2, groups)),
        ],
        compiler_params=pltpu.CompilerParams(vmem_limit_bytes=56 << 20),
        name="attend",
    )(tokens, positions, positions[:, None], freq, gain[None, :], w_q, w_k, w_v, cache_k, cache_v)


from jax.sharding import PartitionSpec as P


def rms_norm(values, gain):
    wide = values.astype(jnp.float32)
    inv_rms = lax.rsqrt(jnp.mean(wide * wide, axis=-1, keepdims=True) + NORM_EPS)
    return (wide * inv_rms * gain.astype(jnp.float32)).astype(jnp.bfloat16)


def solution(mesh):
    sp_size = mesh.shape["sp"]
    cache_spec = P("dp", "sp", "tp", None)
    row_spec = P("dp", None)
    col_spec = P(None, "tp")
    in_specs = (row_spec, P("dp"), cache_spec, cache_spec, P(None), col_spec, col_spec, col_spec, P("tp", None), P(None), col_spec, col_spec, P("tp", None))
    out_specs = (row_spec, cache_spec, cache_spec)

    def local_step(tokens, positions, cache_k, cache_v, attn_gain, w_q, w_k, w_v, w_o, mlp_gain, w_gate, w_up, w_down):
        rows = tokens.shape[0]
        head = cache_k.shape[3]
        heads = w_q.shape[1] // head
        part, new_k, new_v = attend(sp_size, tokens, positions, cache_k, cache_v, attn_gain, w_q, w_k, w_v)
        g = rows // GRP
        o = part[:, :GRP * heads, :].reshape(rows, heads, head)
        st = part[:, GRP * heads:, :128].reshape(g, 8, 8, 16)[..., 0]
        n_pairs = GRP * heads // 8
        st = st.reshape(g, 8, n_pairs, 2).transpose(3, 0, 2, 1).reshape(2, rows, heads)
        m, l = st[0], st[1]
        gm = lax.pmax(m, "sp")
        f = jnp.exp(m - gm)
        packed = jnp.concatenate([o * f[..., None], (l * f)[..., None]], axis=-1)
        total = lax.psum(packed, "sp")
        attended = (total[..., :head] / total[..., head:]).astype(jnp.bfloat16).reshape(rows, heads * head)
        attn_proj = lax.psum(jnp.dot(attended, w_o, preferred_element_type=jnp.float32), "tp")
        hidden = (tokens.astype(jnp.float32) + attn_proj).astype(jnp.bfloat16)
        normed_mlp = rms_norm(hidden, mlp_gain)
        gate_proj = jnp.dot(normed_mlp, w_gate, preferred_element_type=jnp.float32)
        up_proj = jnp.dot(normed_mlp, w_up, preferred_element_type=jnp.float32)
        activated = (jax.nn.silu(gate_proj) * up_proj).astype(jnp.bfloat16)
        mlp_down = lax.psum(jnp.dot(activated, w_down, preferred_element_type=jnp.float32), "tp")
        layer_out = (hidden.astype(jnp.float32) + mlp_down).astype(jnp.bfloat16)
        return layer_out, new_k, new_v

    return jax.shard_map(local_step, mesh=mesh, in_specs=in_specs, out_specs=out_specs, check_vma=False)
```

time: 275 us -> 255 us (0.927)
  other arithmetic: 31.5 us -> 5.6 us
  Pallas kernels: 0 us -> 24.4 us
  matrix products: 58.6 us -> 40.5 us
    pallas_call x0 -> x1, Pallas kernels: none -> 24.4 us  [attend(): pl.pallas_call(functools.partial(attend_kernel, sp_size), out_shape=(jax....]
    select_n x1 -> x0, other arithmetic: 21.5 us -> none  [local_step(): new_v = jnp.where(hit_mask, v_new[:, None], cache_v)]
    dot_general x5 -> x0, matrix products: 18 us -> none  [the longest x1 4.76 us: local_step(): jnp.dot(normed, w_q, preferred_element_type=jnp.float32)]
    unnamed x8 -> x6, local copies, waits for them, and re-layouts: 3.41 us -> 0.48 us
where the time goes in v1:
time: 255 us; the launch traced here: 253 us
  waiting for transfers between devices  138 us (54%)
  matrix products  40.5 us (16%)
  Pallas kernels  24.4 us (10%)
  blocking collectives  24.1 us (9%)
  between operations  13.9 us (5%)
  local copies, waits for them, and re-layouts  6.86 us (3%)
  other arithmetic  5.6 us (2%)
    psum x1, waiting for transfers between devices, local_step(): total = lax.psum(packed, 'sp')  56.8 us
    psum x1, waiting for transfers between devices, local_step(): lax.psum(jnp.dot(activated, w_down, preferred_element_type=jnp.float32),...  41.4 us
    psum x1, waiting for transfers between devices, local_step(): lax.psum(jnp.dot(attended, w_o, preferred_element_type=jnp.float32), 'tp')  39.5 us
    pallas_call x1, Pallas kernels, attend(): pl.pallas_call(functools.partial(attend_kernel, sp_size), out_shape=(jax....  24.4 us
    pmax x1, blocking collectives, local_step(): gm = lax.pmax(m, 'sp')  24.1 us
    dot_general x1, matrix products, local_step(): jnp.dot(activated, w_down, preferred_element_type=jnp.float32)  22.7 us
    dot_general x1, matrix products, local_step(): gate_proj = jnp.dot(normed_mlp, w_gate, preferred_element_type=jnp.float32)  12.1 us
    dot_general x1, matrix products, local_step(): jnp.dot(attended, w_o, preferred_element_type=jnp.float32)  5.71 us
  transfers between devices with their start and end apart: 3, of which 3 were waited for; matrix products, arithmetic and copies ran while one was open for 0% of the time, Pallas kernels for 0%

profile of v1, /device:TPU:97, one launch (start us, length us, event | category | flops | bytes accessed | tf_op | source)
XLA Modules:
  0.0 253.5 jit_solution(10794005560162937805)
XLA Ops:
  7.2 0.0 copy-start
  7.2 0.0 copy-start.1
  7.2 0.1 all-reduce.4.cloned.1.call-start
  7.3 1.3 broadcast_in_dim.17.gain_ref
  8.6 1.4 copy.27.posv_ref
  9.9 24.4 %attend.1 = (f32[8,40,256]{2,1,0:T(8,128)}, bf16[64,128,2,256]{3,2,1,0:T(2,128)(2,1)}, bf16[64,128,2,256]{3,2,1,0:T(2,128)(2,1)}) custom-call(bf16[64,3840]{1,0:T(8,128)(2,1)} %tok_ref.1, s32[64]{0:T(128)} %pos_ref.1, s32[64,1]{1,0:T(8,128)} %copy.27.posv_ref, f32[1,128]{1,0:T(1,128)} %constant.15.freq_ref, bf16[1,3840]{1,0:T(2,128)(2,1)} %broadcast_in_dim.17.gain_ref, ...), custom_call_target="tpu_custom_call" | custom-call | tf_op jit(solution)/shard_map/attend/pallas_call | solution.py:153
  34.4 0.8 slice.24
  35.1 1.0 slice.23
  36.1 0.1 reshape.30
  36.2 0.1 reshape.31
  36.3 0.5 copy.37
  36.8 0.1 squeeze.6
  36.9 0.1 squeeze.7
  37.0 24.1 %pmax.7 = f32[64,4]{1,0:T(8,128)S(1)} all-reduce(f32[64,4]{1,0:T(8,128)S(1)} %squeeze.6), channel_id=1, replica_groups=mesh['dp'=1,'tp'=4,'sp'=8] {'sp'}, use_global_device_ids=true, to_apply=%region_0.0 | all-reduce | flops 256 | bytes 2048 | tf_op jit(solution)/shard_map/pmax | solution.py:200
  61.1 0.5 copy.32
  61.6 0.1 broadcast_multiply_fusion
  61.7 0.8 pad_maximum_fusion
  62.5 0.1 all-reduce.4.cloned.1.call-update
  62.6 0.1 all-reduce.6.cloned.1.call-start
  62.7 56.8 %all-reduce.4.cloned.1.call-done = f32[64,4,257]{2,1,0:T(4,128)} async-done(((f32[64,4,257]{2,1,0:T(4,128)}), f32[64,4,257]{2,1,0:T(4,128)}) %all-reduce.4.cloned.1.call-update) | async-done | bytes 263184 | tf_op jit(solution)/shard_map/psum | solution.py:203
  119.4 0.9 slice.34
  120.3 0.1 copy.33
  120.4 0.1 copy.34
  120.5 1.1 fusion.12
  121.7 5.7 %fusion.19 = f32[64,3840]{1,0:T(8,128)} fusion(bf16[64,1024]{1,0:T(8,128)(2,1)S(1)} %bitcast.16, bf16[1024,3840]{1,0:T(8,128)(2,1)} %param.22), kind=kOutput, calls=%fused_computation.27 | convolution fusion | flops 503316480 | bytes 8978432 | tf_op jit(solution)/shard_map/dot_general | solution.py:205
  127.4 0.1 all-reduce.6.cloned.1.call-update
  127.5 0.1 all-reduce.8.cloned.1.call-start
  127.5 0.0 copy-done.1
  127.5 39.5 %all-reduce.6.cloned.1.call-done = f32[64,3840]{1,0:T(8,128)} async-done(((f32[64,3840]{1,0:T(8,128)}), f32[64,3840]{1,0:T(8,128)}) %all-reduce.6.cloned.1.call-update) | async-done | bytes 983056 | tf_op jit(solution)/shard_map/psum | solution.py:205
  167.1 0.0 copy-done
  167.1 1.4 fusion.2
  168.5 12.1 %fusion.15 = f32[64,3840]{1,0:T(8,128)S(1)} fusion(bf16[3840,3840]{1,0:T(8,128)(2,1)} %param.24, bf16[64,3840]{1,0:T(8,128)(2,1)S(1)} %get-tuple-element.10, f32[3840]{0:T(1024)S(1)} %convert_element_type.29, f32[64]{0:T(128)S(1)} %add_rsqrt_fusion), kind=kOutput, calls=%fused_computation.20 | convolution fusion | flops 1888419840 | bytes 30981376 | tf_op jit(solution)/shard_map/dot_general | solution.py:208
  180.7 22.7 %fusion.1 = f32[64,3840]{1,0:T(8,128)} fusion(bf16[3840,3840]{1,0:T(8,128)(2,1)} %param.26, bf16[3840,3840]{1,0:T(8,128)(2,1)} %param.25, f32[64,3840]{1,0:T(8,128)S(1)} %fusion.15, bf16[64,3840]{1,0:T(8,128)(2,1)S(1)} %get-tuple-element.10, f32[3840]{0:T(1024)S(1)} %convert_element_type.29, f32[64]{0:T(128)S(1)} %add_rsqrt_fusion), kind=kOutput, calls=%fused_computation.2 | convolution fusion | flops 3777331200 | bytes 61455616 | tf_op jit(solution)/shard_map/dot_general | solution.py:211
  203.4 0.1 all-reduce.8.cloned.1.call-update
  203.5 41.4 %all-reduce.8.cloned.1.call-done = f32[64,3840]{1,0:T(8,128)} async-done(((f32[64,3840]{1,0:T(8,128)}), f32[64,3840]{1,0:T(8,128)}) %all-reduce.8.cloned.1.call-update) | async-done | bytes 983056 | tf_op jit(solution)/shard_map/psum | solution.py:211
  244.9 2.1 fusion.5
  (7 shorter events, 0.1 us)
Async XLA Ops:
  7.2 159.9 %copy-start = (bf16[64,3840]{1,0:T(8,128)(2,1)S(1)}, bf16[64,3840]{1,0:T(8,128)(2,1)}, u32[]{:S(2)}) copy-start(bf16[64,3840]{1,0:T(8,128)(2,1)} %tok_ref.1) | copy-start | bytes 1474564
  7.2 120.3 %copy-start.1 = (bf16[3840]{0:T(1024)(128)(2,1)S(1)}, bf16[3840]{0:T(1024)(128)(2,1)}, u32[]{:S(2)}) copy-start(bf16[3840]{0:T(1024)(128)(2,1)} %param.23) | copy-start | bytes 23044
  7.2 112.2 %all-reduce.4.cloned.1.call-start = ((), (), s32[]{:S(2)}) async-start(), calls=%async_computation | async-start | bytes 786432 | tf_op jit(solution)/shard_map/psum | solution.py:203
  62.6 104.5 %all-reduce.6.cloned.1.call-start = ((), (), s32[]{:S(2)}) async-start(), calls=%async_computation.1 | async-start | bytes 1966080 | tf_op jit(solution)/shard_map/psum | solution.py:205
  127.5 117.4 %all-reduce.8.cloned.1.call-start = ((), (), s32[]{:S(2)}) async-start(), calls=%async_computation.2 | async-start | bytes 1966080 | tf_op jit(solution)/shard_map/psum | solution.py:211
Sparse Core Ops, SparseCore 0:
  62.7 56.6 all-reduce.3
  127.6 39.4 all-reduce.5
  203.6 41.2 all-reduce.7

commit v2 on v1

--- a/solution.py
+++ b/solution.py
@@ -169,17 +169,302 @@
     )(tokens, positions, positions[:, None], freq, gain[None, :], w_q, w_k, w_v, cache_k, cache_v)
 
 
+MESH_ID = pl.DeviceIdType.MESH
+CHUNK = 1024
+CORES = 2
+
+
+def finish_kernel(sp_size, tp_size, part_ref, tok_ref, gain_ref, wo_hbm, wg_hbm, wu_hbm, wd_hbm, out_ref,
+                  wo, wg, wu, wd, crecv, att, toks, dsend, drecv, hbuf, normed, hidden_mlp, dpart, precv, gsum, g1recv, s1, g2recv, obuf,
+                  wsem, csem, dsem, asem, bsem, psem, g1sem, g2sem):
+    f32, bf = jnp.float32, jnp.bfloat16
+    rows, width = tok_ref.shape
+    n_x = sp_size // CORES
+    heads_cols = wo.shape[0]
+    mlp_cols = wg.shape[1]
+    sp, tp = lax.axis_index("sp"), lax.axis_index("tp")
+    x, core = sp // CORES, sp % CORES
+    flip = 1 - core
+    group = rows // sp_size
+
+    def rc(src, dst, ssem, rsem, to_sp, to_tp):
+        return pltpu.make_async_remote_copy(src_ref=src, dst_ref=dst, send_sem=ssem, recv_sem=rsem,
+                                            device_id={"sp": to_sp, "tp": to_tp}, device_id_type=MESH_ID)
+
+    blocks = wg_hbm.shape[1] // 128
+    per = mlp_cols // 128
+    first = jnp.minimum(sp * per, blocks - per)
+    cols = pl.ds(pl.multiple_of(first * 128, 128), mlp_cols)
+    loads = [pltpu.make_async_copy(wo_hbm, wo.at[:, pl.ds(0, width)], wsem.at[0]),
+             pltpu.make_async_copy(wg_hbm.at[:, cols], wg, wsem.at[1]),
+             pltpu.make_async_copy(wu_hbm.at[:, cols], wu, wsem.at[2]),
+             pltpu.make_async_copy(wd_hbm.at[cols, :], wd.at[:, pl.ds(0, width)], wsem.at[3])]
+    for cp in loads:
+        cp.start()
+
+    barrier = pltpu.get_barrier_semaphore()
+    for k in range(1, sp_size):
+        pl.semaphore_signal(barrier, inc=1, device_id={"sp": (sp + k) % sp_size, "tp": tp}, device_id_type=MESH_ID)
+    for k in range(1, tp_size):
+        pl.semaphore_signal(barrier, inc=1, device_id={"sp": sp, "tp": (tp + k) % tp_size}, device_id_type=MESH_ID)
+    pl.semaphore_wait(barrier, sp_size + tp_size - 2)
+
+    def part_copy(k):
+        to = (sp + k) % sp_size
+        return rc(part_ref.at[to], crecv.at[sp], csem.at[0, k - 1], csem.at[1, k - 1], to, tp)
+
+    for k in range(1, sp_size):
+        part_copy(k).start()
+    pad = CHUNK * tp_size - width
+    wo[:, width:] = jnp.zeros((heads_cols, pad), bf)
+    wd[:, width:] = jnp.zeros((mlp_cols, pad), bf)
+    for t in range(tp_size):
+        w = min(CHUNK, width - t * CHUNK)
+        toks[:, t, :, :w] = tok_ref[:, t * CHUNK:t * CHUNK + w].astype(f32).reshape(sp_size, group, w)
+        if w < CHUNK:
+            toks[:, t, :, w:] = jnp.zeros((sp_size, group, CHUNK - w), f32)
+    crecv[sp] = part_ref[sp]
+    for k in range(1, sp_size):
+        src = (sp + sp_size - k) % sp_size
+        rc(crecv.at[src], crecv.at[src], csem.at[0, k - 1], csem.at[1, k - 1], sp, tp).wait_recv()
+
+    n_rows = part_ref.shape[1] - 8
+    n_pairs = n_rows // 8
+    span = 128 // (2 * n_pairs)
+    head = part_ref.shape[2]
+    heads = heads_cols // head
+    stats = [crecv[i, n_rows:, :128] for i in range(sp_size)]
+    top = functools.reduce(jnp.maximum, stats)
+    factors = [jnp.exp(st - top) for st in stats]
+    for j in range(n_pairs):
+        lo = 2 * j * span
+        num, den = None, None
+        for i in range(sp_size):
+            f = factors[i][:, lo:lo + 1]
+            o = crecv[i, j * 8:(j + 1) * 8, :] * f
+            l = stats[i][:, lo + span:lo + span + 1] * f
+            num, den = (o, l) if num is None else (num + o, den + l)
+        o = num / den
+        att[0, j * 8:(j + 1) * 8, :] = o[:, :head // 2]
+        att[1, j * 8:(j + 1) * 8, :] = o[:, head // 2:]
+    attended = jnp.concatenate([att[half, pl.ds(h, group, stride=heads), :] for h in range(heads) for half in range(2)], axis=-1).astype(bf)
+
+    loads[0].wait()
+
+    def proj_copy(k):
+        to = (tp + k) % tp_size
+        return rc(dsend.at[to], drecv.at[k - 1], dsem.at[0, k - 1], dsem.at[1, k - 1], sp, to)
+
+    order = (1, 3, 2) if tp_size == 4 else tuple(range(1, tp_size))
+    for k in order + (0,):
+        t = (tp + k) % tp_size
+        dsend[t] = jnp.dot(attended, wo[:, pl.ds(pl.multiple_of(t * CHUNK, CHUNK), CHUNK)], preferred_element_type=f32)
+        if k:
+            proj_copy(k).start()
+    total = toks[sp, tp] + dsend[tp]
+    mine = dsend[tp]
+    for k in order:
+        rc(drecv.at[k - 1], drecv.at[k - 1], dsem.at[0, k - 1], dsem.at[1, k - 1], sp, tp).wait_recv()
+        mine = mine + drecv[k - 1]
+    hbuf[sp, tp] = (toks[sp, tp] + mine).astype(bf).astype(f32)
+
+    def gather(buf, which):
+        def chunk(s, t):
+            return buf.at[s, t]
+
+        def own_chunk(d_sp, d_tp, c, k, j):
+            s = (d_sp + sp_size - CORES * (k * (1 - c) + j * c)) % sp_size
+            t = (d_tp + tp_size - (k * c + j * (1 - c))) % tp_size
+            return s, t
+
+        def first_copy(k):
+            return rc(chunk(sp, tp), chunk(sp, tp), asem.at[which, 0, k - 1], asem.at[which, 1, k - 1],
+                      (sp + CORES * k * core) % sp_size, (tp + k * flip) % tp_size)
+
+        def second_copy(k, j):
+            s, t = own_chunk(sp, tp, core, 0, j)
+            return rc(chunk(s, t), chunk(s, t), bsem.at[which, 0, k - 1, j], bsem.at[which, 1, k - 1, j],
+                      (sp + CORES * k * flip) % sp_size, (tp + k * core) % tp_size)
+
+        partner = sp + 1 - 2 * core
+
+        def pair_copy(k, j):
+            s, t = own_chunk(sp, tp, core, k, j)
+            return rc(chunk(s, t), chunk(s, t), psem.at[which, 0, k, j], psem.at[which, 1, k, j], partner, tp)
+
+        for k in order:
+            first_copy(k).start()
+        for k in order:
+            second_copy(k, 0).start()
+        pair_copy(0, 0).start()
+        for j in order:
+            s, t = own_chunk(sp, tp, core, 0, j)
+            rc(chunk(s, t), chunk(s, t), asem.at[which, 0, j - 1], asem.at[which, 1, j - 1], sp, tp).wait_recv()
+            for k in order:
+                second_copy(k, j).start()
+            pair_copy(0, j).start()
+        for j in (0,) + order:
+            for k in order:
+                s, t = own_chunk(sp, tp, core, k, j)
+                rc(chunk(s, t), chunk(s, t), bsem.at[which, 0, k - 1, j], bsem.at[which, 1, k - 1, j], sp, tp).wait_recv()
+                pair_copy(k, j).start()
+        for j in (0,) + order:
+            for k in (0,) + order:
+                s, t = own_chunk(partner, tp, flip, k, j)
+                rc(chunk(s, t), chunk(s, t), psem.at[which, 0, k, j], psem.at[which, 1, k, j], sp, tp).wait_recv()
+        for k in order:
+            first_copy(k).wait_send()
+            for j in range(tp_size):
+                second_copy(k, j).wait_send()
+        for k in range(n_x):
+            for j in range(tp_size):
+                pair_copy(k, j).wait_send()
+
+    gather(hbuf, 0)
+
+    square = None
+    for t in range(tp_size):
+        w = min(CHUNK, width - t * CHUNK)
+        v = hbuf[:, t].reshape(rows, CHUNK)[:, :w]
+        s = jnp.sum(v * v, axis=-1, keepdims=True)
+        square = s if square is None else square + s
+    inv = lax.rsqrt(square / width + NORM_EPS)
+    for t in range(tp_size):
+        w = min(CHUNK, width - t * CHUNK)
+        v = hbuf[:, t].reshape(rows, CHUNK)[:, :w]
+        normed[:, t * CHUNK:t * CHUNK + w] = (v * inv * gain_ref[:, t * CHUNK:t * CHUNK + w].astype(f32)).astype(bf)
+    loads[1].wait()
+    gate = jnp.dot(normed[...], wg[...], preferred_element_type=f32)
+    loads[2].wait()
+    up = jnp.dot(normed[...], wu[...], preferred_element_type=f32)
+    block = first + lax.broadcasted_iota(jnp.int32, (rows, mlp_cols), 1) // 128
+    hidden_mlp[...] = jnp.where(block >= sp * per, jax.nn.silu(gate) * up, 0.0).astype(bf)
+    loads[3].wait()
+
+    partner = sp + 1 - 2 * core
+
+    def half_copy(t):
+        return rc(dpart.at[:, flip, t], precv.at[:, t], psem.at[2, 0, 0, t], psem.at[2, 1, 0, t], partner, tp)
+
+    steps = order + (0,)
+    for i in steps:
+        t = (tp + i) % tp_size
+        part = jnp.dot(hidden_mlp[...], wd[:, pl.ds(pl.multiple_of(t * CHUNK, CHUNK), CHUNK)], preferred_element_type=f32)
+        dpart[:, :, t] = part.reshape(n_x, CORES, group, CHUNK)
+        half_copy(t).start()
+
+    def x_copy(k, t):
+        to = (x + k) % n_x
+        return rc(gsum.at[to, t], g1recv.at[k - 1, t], g1sem.at[0, k - 1, t], g1sem.at[1, k - 1, t], CORES * to + core, tp)
+
+    def y_copy(k, j):
+        to = (tp + k) % tp_size
+        return rc(gsum.at[j, to], g1recv.at[k - 1, j], g1sem.at[0, k - 1, j], g1sem.at[1, k - 1, j], sp, to)
+
+    for i in steps:
+        t = (tp + i) % tp_size
+        rc(precv.at[:, t], precv.at[:, t], psem.at[2, 0, 0, t], psem.at[2, 1, 0, t], sp, tp).wait_recv()
+        gsum[:, t] = dpart[:, core, t] + precv[:, t]
+
+        @pl.when(core == 0)
+        def _():
+            for k in order:
+                x_copy(k, t).start()
+
+        if i:
+            @pl.when(core == 1)
+            def _():
+                for j in range(n_x):
+                    y_copy(i, j).start()
+
+    b_own = tp * flip + x * core
+
+    def b_copy(k):
+        b = (b_own + k) % tp_size
+        return rc(s1.at[b], g2recv.at[k - 1], g2sem.at[0, k - 1], g2sem.at[1, k - 1],
+                  (sp + CORES * k * core) % sp_size, (tp + k * flip) % tp_size)
+
+    for k in steps:
+        b = (b_own + k) % tp_size
+        acc = gsum[x * flip + b * core, b * flip + tp * core]
+        for a in order:
+            rc(g1recv.at[a - 1, b], g1recv.at[a - 1, b], g1sem.at[0, a - 1, b], g1sem.at[1, a - 1, b], sp, tp).wait_recv()
+            acc = acc + g1recv[a - 1, b]
+        s1[b] = acc
+        if k:
+            b_copy(k).start()
+    acc = s1[b_own]
+    for k in order:
+        rc(g2recv.at[k - 1], g2recv.at[k - 1], g2sem.at[0, k - 1], g2sem.at[1, k - 1], sp, tp).wait_recv()
+        acc = acc + g2recv[k - 1]
+    obuf[sp, tp] = (hbuf[sp, tp] + acc).astype(bf).astype(f32)
+
+    gather(obuf, 1)
+    for t in range(tp_size):
+        w = min(CHUNK, width - t * CHUNK)
+        out_ref[:, t * CHUNK:t * CHUNK + w] = obuf[:, t].reshape(rows, CHUNK)[:, :w].astype(bf)
+
+    for k in range(1, sp_size):
+        part_copy(k).wait_send()
+    for k in order:
+        proj_copy(k).wait_send()
+        b_copy(k).wait_send()
+    for t in range(tp_size):
+        half_copy(t).wait_send()
+
+    @pl.when(core == 0)
+    def _():
+        for k in order:
+            for t in range(tp_size):
+                x_copy(k, t).wait_send()
+
+    @pl.when(core == 1)
+    def _():
+        for k in order:
+            for j in range(n_x):
+                y_copy(k, j).wait_send()
+
+
+def finish(sp_size, tp_size, part, tokens, gain, w_o, w_gate, w_up, w_down):
+    rows, width = tokens.shape
+    group = rows // sp_size
+    n_x = sp_size // CORES
+    blocks = w_gate.shape[1] // 128
+    mlp_cols = -(-blocks // sp_size) * 128
+    padded = CHUNK * tp_size
+    f32, bf = jnp.float32, jnp.bfloat16
+    any_spec = pl.BlockSpec(memory_space=pl.ANY)
+    vm = pl.BlockSpec(memory_space=pltpu.VMEM)
+    dma = pltpu.SemaphoreType.DMA
+    head = part.shape[2]
+    return pl.pallas_call(
+        functools.partial(finish_kernel, sp_size, tp_size),
+        out_shape=jax.ShapeDtypeStruct((rows, width), bf),
+        in_specs=[vm, vm, vm] + [any_spec] * 4,
+        out_specs=vm,
+        scratch_shapes=[
+            pltpu.VMEM((w_o.shape[0], padded), bf), pltpu.VMEM((width, mlp_cols), bf), pltpu.VMEM((width, mlp_cols), bf), pltpu.VMEM((mlp_cols, padded), bf),
+            pltpu.VMEM(part.shape, f32), pltpu.VMEM((2, part.shape[1] - 8, head // 2), f32),
+            pltpu.VMEM((sp_size, tp_size, group, CHUNK), f32),
+            pltpu.VMEM((tp_size, group, CHUNK), f32), pltpu.VMEM((tp_size - 1, group, CHUNK), f32),
+            pltpu.VMEM((sp_size, tp_size, group, CHUNK), f32),
+            pltpu.VMEM((rows, width), bf), pltpu.VMEM((rows, mlp_cols), bf),
+            pltpu.VMEM((n_x, CORES, tp_size, group, CHUNK), f32), pltpu.VMEM((n_x, tp_size, group, CHUNK), f32), pltpu.VMEM((n_x, tp_size, group, CHUNK), f32),
+            pltpu.VMEM((3, tp_size, group, CHUNK), f32), pltpu.VMEM((tp_size, group, CHUNK), f32), pltpu.VMEM((3, group, CHUNK), f32),
+            pltpu.VMEM((sp_size, tp_size, group, CHUNK), f32),
+            dma((4,)), dma((2, sp_size - 1)), dma((2, tp_size - 1)), dma((2, 2, 3)), dma((2, 2, 3, tp_size)), dma((3, 2, n_x, tp_size)),
+            dma((2, 3, tp_size)), dma((2, 3)),
+        ],
+        compiler_params=pltpu.CompilerParams(vmem_limit_bytes=56 << 20, collective_id=0, has_side_effects=True),
+        name="finish",
+    )(part, tokens, gain[None, :], w_o, w_gate, w_up, w_down)
+
+
 from jax.sharding import PartitionSpec as P
 
 
-def rms_norm(values, gain):
-    wide = values.astype(jnp.float32)
-    inv_rms = lax.rsqrt(jnp.mean(wide * wide, axis=-1, keepdims=True) + NORM_EPS)
-    return (wide * inv_rms * gain.astype(jnp.float32)).astype(jnp.bfloat16)
-
-
 def solution(mesh):
-    sp_size = mesh.shape["sp"]
+    sp_size, tp_size = mesh.shape["sp"], mesh.shape["tp"]
     cache_spec = P("dp", "sp", "tp", None)
     row_spec = P("dp", None)
     col_spec = P(None, "tp")
@@ -187,29 +472,8 @@
     out_specs = (row_spec, cache_spec, cache_spec)
 
     def local_step(tokens, positions, cache_k, cache_v, attn_gain, w_q, w_k, w_v, w_o, mlp_gain, w_gate, w_up, w_down):
-        rows = tokens.shape[0]
-        head = cache_k.shape[3]
-        heads = w_q.shape[1] // head
         part, new_k, new_v = attend(sp_size, tokens, positions, cache_k, cache_v, attn_gain, w_q, w_k, w_v)
-        g = rows // GRP
-        o = part[:, :GRP * heads, :].reshape(rows, heads, head)
-        st = part[:, GRP * heads:, :128].reshape(g, 8, 8, 16)[..., 0]
-        n_pairs = GRP * heads // 8
-        st = st.reshape(g, 8, n_pairs, 2).transpose(3, 0, 2, 1).reshape(2, rows, heads)
-        m, l = st[0], st[1]
-        gm = lax.pmax(m, "sp")
-        f = jnp.exp(m - gm)
-        packed = jnp.concatenate([o * f[..., None], (l * f)[..., None]], axis=-1)
-        total = lax.psum(packed, "sp")
-        attended = (total[..., :head] / total[..., head:]).astype(jnp.bfloat16).reshape(rows, heads * head)
-        attn_proj = lax.psum(jnp.dot(attended, w_o, preferred_element_type=jnp.float32), "tp")
-        hidden = (tokens.astype(jnp.float32) + attn_proj).astype(jnp.bfloat16)
-        normed_mlp = rms_norm(hidden, mlp_gain)
-        gate_proj = jnp.dot(normed_mlp, w_gate, preferred_element_type=jnp.float32)
-        up_proj = jnp.dot(normed_mlp, w_up, preferred_element_type=jnp.float32)
-        activated = (jax.nn.silu(gate_proj) * up_proj).astype(jnp.bfloat16)
-        mlp_down = lax.psum(jnp.dot(activated, w_down, preferred_element_type=jnp.float32), "tp")
-        layer_out = (hidden.astype(jnp.float32) + mlp_down).astype(jnp.bfloat16)
+        layer_out = finish(sp_size, tp_size, part, tokens, mlp_gain, w_o, w_gate, w_up, w_down)
         return layer_out, new_k, new_v
 
     return jax.shard_map(local_step, mesh=mesh, in_specs=in_specs, out_specs=out_specs, check_vma=False)

time: 255 us -> 85.7 us (0.34)
  waiting for transfers between devices: 138 us -> 0 us
  Pallas kernels: 24.4 us -> 78.9 us
  matrix products: 40.5 us -> 0 us
  blocking collectives: 24.1 us -> 0 us
  between operations: 13.9 us -> 0.65 us
  other arithmetic: 5.6 us -> 0 us
    psum x3 -> x0, waiting for transfers between devices: 138 us -> none  [the longest x1 56.8 us: local_step(): total = lax.psum(packed, 'sp')]
    pallas_call x0 -> x1, Pallas kernels: none -> 54.5 us  [finish(): pl.pallas_call(functools.partial(finish_kernel, sp_size, tp_size), out_sh...]
    dot_general x3 -> x0, matrix products: 40.5 us -> none  [the longest x1 22.7 us: local_step(): jnp.dot(activated, w_down, preferred_element_type=jnp.float32)]
    pmax x1 -> x0, blocking collectives: 24.1 us -> none  [local_step(): gm = lax.pmax(m, 'sp')]
    convert_element_type x3 -> x0, other arithmetic: 3.17 us -> none  [the longest x1 2.06 us: local_step(): layer_out = (hidden.astype(jnp.float32) + mlp_down).astype(jnp.bfloat16)]
    slice x7 -> x0, local copies, waits for them, and re-layouts: 2.76 us -> none  [the longest x2 1.01 us: local_step(): total[..., head:]]
  transfers between devices with their start and end apart: 3 -> 0, of which waited for: 3 -> 0; matrix products, arithmetic and copies ran while one was open for 0% -> 0% of each run, Pallas kernels for 0% -> 0%
where the time goes in v2:
time: 85.7 us; the launch traced here: 85.4 us
  Pallas kernels  78.9 us (92%)
  local copies, waits for them, and re-layouts  5.81 us (7%)
    pallas_call x1, Pallas kernels, finish(): pl.pallas_call(functools.partial(finish_kernel, sp_size, tp_size), out_sh...  54.5 us
    pallas_call x1, Pallas kernels, attend(): pl.pallas_call(functools.partial(attend_kernel, sp_size), out_shape=(jax....  24.4 us
    unnamed x1, local copies, waits for them, and re-layouts  1.84 us

profile of v2, /device:TPU:97, one launch (start us, length us, event | category | flops | bytes accessed | tf_op | source)
XLA Modules:
  0.0 85.4 jit_solution(13541863507248026078)
XLA Ops:
  0.6 1.3 %broadcast_in_dim.14.gain_ref = bf16[1,3840]{1,0:T(2,128)(2,1)} reshape(bf16[3840]{0:T(1024)(128)(2,1)} %param.18) | data formatting | bytes 15360 | tf_op jit(solution)/shard_map/broadcast_in_dim | solution.py:169
  1.9 1.3 %broadcast_in_dim.15.gain_ref = bf16[1,3840]{1,0:T(2,128)(2,1)} reshape(bf16[3840]{0:T(1024)(128)(2,1)} %param.23) | data formatting | bytes 15360 | tf_op jit(solution)/shard_map/broadcast_in_dim | solution.py:460
  3.2 1.4 %copy.17.posv_ref = s32[64,1]{1,0:T(8,128)} copy(s32[64,1]{0,1:T(1,128)} %bitcast.1) | data formatting | bytes 512 | tf_op jit(solution)/shard_map/broadcast_in_dim | solution.py:169
  4.6 24.4 %attend.1 = (f32[8,40,256]{2,1,0:T(8,128)}, bf16[64,128,2,256]{3,2,1,0:T(2,128)(2,1)}, bf16[64,128,2,256]{3,2,1,0:T(2,128)(2,1)}) custom-call(bf16[64,3840]{1,0:T(8,128)(2,1)} %tok_ref.3, s32[64]{0:T(128)} %pos_ref.1, s32[64,1]{1,0:T(8,128)} %copy.17.posv_ref, f32[1,128]{1,0:T(1,128)} %constant.5.freq_ref, bf16[1,3840]{1,0:T(2,128)(2,1)} %broadcast_in_dim.14.gain_ref, ...), custom_call_target="tpu_custom_call" | custom-call | tf_op jit(solution)/shard_map/attend/pallas_call | solution.py:153
  29.0 54.5 %finish.1 = bf16[64,3840]{1,0:T(8,128)(2,1)} custom-call(f32[8,40,256]{2,1,0:T(8,128)} %get-tuple-element.6.part_ref, bf16[64,3840]{1,0:T(8,128)(2,1)} %tok_ref.3, bf16[1,3840]{1,0:T(2,128)(2,1)} %broadcast_in_dim.15.gain_ref, bf16[1024,3840]{1,0:T(8,128)(2,1)} %wo_hbm.1, bf16[3840,3840]{1,0:T(8,128)(2,1)} %wg_hbm.1, bf16[3840,3840]{1,0:T(8,128)(2,1)} %wu_hbm.1, ...), custom_call_target="tpu_custom_call" | custom-call | tf_op jit(solution)/shard_map/finish/pallas_call | solution.py:440
  83.5 1.8 %copy.19 = bf16[64,3840]{1,0:T(8,128)(2,1)} copy(bf16[64,3840]{1,0:T(8,128)(2,1)} %finish.1) | data formatting | bytes 983040

commit v3 on v2

--- a/solution.py
+++ b/solution.py
@@ -8,11 +8,12 @@
 ROPE_THETA = 10000.0
 GRP = 8
 KSTEP = 768
-
-
-def attend_kernel(sp_size, tok_ref, pos_ref, posv_ref, freq_ref, gain_ref, wq_hbm, wk_hbm, wv_hbm, ck_hbm, cv_hbm,
+EARLY = 2
+
+
+def attend_kernel(sp_size, tok_ref, pos_ref, freq_ref, gain_ref, wq_hbm, wk_hbm, wv_hbm, ck_hbm, cv_hbm,
                   part_ref, nk_hbm, nv_hbm,
-                  wq, wk, wv, kbuf, vbuf, acc, normed, qrows, knew, vnew, wsem, csem, osem):
+                  wq, wk, wv, kbuf, vbuf, acc, normed, qrows, knew, vnew, posrow, wsem, csem, osem):
     rows, width = tok_ref.shape
     slots_local = kbuf.shape[1]
     kv_heads = kbuf.shape[2]
@@ -43,14 +44,12 @@
     for c in range(ksteps):
         for cp in wcopies(c):
             cp.start()
-    for g in range(groups):
-        for cp in ccopies(g):
-            cp.start()
-
     wide = tok_ref[...].astype(jnp.float32)
     inv = lax.rsqrt(jnp.mean(wide * wide, axis=-1, keepdims=True) + NORM_EPS)
-    normed[...] = (wide * inv * gain_ref[...].astype(jnp.float32)).astype(jnp.bfloat16)
-    angles = posv_ref[...].astype(jnp.float32) * freq_ref[...]
+    normed[...] = (wide * inv * gain_ref[...].astype(jnp.float32).reshape(1, width)).astype(jnp.bfloat16)
+    for b in range(rows):
+        posrow[b:b + 1, :] = jnp.full((1, half), pos_ref[b], jnp.int32)
+    angles = posrow[...].astype(jnp.float32) * freq_ref[...]
     cos, sin = jnp.cos(angles), jnp.sin(angles)
     acc[...] = jnp.zeros_like(acc)
 
@@ -58,6 +57,14 @@
     def _(c):
         for cp in wcopies(c):
             cp.wait()
+
+        for at, these in ((ksteps - 2, range(EARLY)), (ksteps - 1, range(EARLY, groups))):
+            @pl.when(c == at)
+            def _():
+                for g in these:
+                    for cp in ccopies(g):
+                        cp.start()
+
         sl = pl.ds(pl.multiple_of(c * KSTEP, KSTEP), KSTEP)
         lhs = normed[:, sl]
         for w, off, cols in ((wq, 0, q_cols), (wk, q_cols, k_cols), (wv, q_cols + k_cols, k_cols)):
@@ -154,7 +161,7 @@
         functools.partial(attend_kernel, sp_size),
         out_shape=(jax.ShapeDtypeStruct((groups, chunk_rows, head), jnp.float32),
                    jax.ShapeDtypeStruct(cache_k.shape, bf), jax.ShapeDtypeStruct(cache_v.shape, bf)),
-        in_specs=[vm, pl.BlockSpec(memory_space=pltpu.SMEM), vm, vm, vm] + [any_spec] * 5,
+        in_specs=[vm, pl.BlockSpec(memory_space=pltpu.SMEM), vm, vm] + [any_spec] * 5,
         out_specs=(vm, any_spec, any_spec),
         scratch_shapes=[
             pltpu.VMEM(w_q.shape, bf), pltpu.VMEM(w_k.shape, bf), pltpu.VMEM(w_v.shape, bf),
@@ -162,11 +169,12 @@
             pltpu.VMEM((rows, qkv_cols), jnp.float32), pltpu.VMEM((rows, width), bf),
             pltpu.VMEM((2, rows * heads, head // 2), jnp.float32),
             pltpu.VMEM((rows, kv_heads, head), jnp.float32), pltpu.VMEM((rows, kv_heads, head), jnp.float32),
+            pltpu.VMEM((rows, head // 2), jnp.int32),
             pltpu.SemaphoreType.DMA((3, width // KSTEP)), pltpu.SemaphoreType.DMA((2, groups)), pltpu.SemaphoreType.DMA((2, groups)),
         ],
         compiler_params=pltpu.CompilerParams(vmem_limit_bytes=56 << 20),
         name="attend",
-    )(tokens, positions, positions[:, None], freq, gain[None, :], w_q, w_k, w_v, cache_k, cache_v)
+    )(tokens, positions, freq, gain, w_q, w_k, w_v, cache_k, cache_v)
 
 
 MESH_ID = pl.DeviceIdType.MESH
@@ -175,8 +183,8 @@
 
 
 def finish_kernel(sp_size, tp_size, part_ref, tok_ref, gain_ref, wo_hbm, wg_hbm, wu_hbm, wd_hbm, out_ref,
-                  wo, wg, wu, wd, crecv, att, toks, dsend, drecv, hbuf, normed, hidden_mlp, dpart, precv, gsum, g1recv, s1, g2recv, obuf,
-                  wsem, csem, dsem, asem, bsem, psem, g1sem, g2sem):
+                  wo, wg, wu, wd, crecv, att, toks, dsend, drecv, hbuf, normed, hidden_mlp, dpart, precv, gsum, grecv, obuf,
+                  wsem, csem, dsem, hsem, qsem, gsem, asem, bsem, psem):
     f32, bf = jnp.float32, jnp.bfloat16
     rows, width = tok_ref.shape
     n_x = sp_size // CORES
@@ -191,16 +199,17 @@
         return pltpu.make_async_remote_copy(src_ref=src, dst_ref=dst, send_sem=ssem, recv_sem=rsem,
                                             device_id={"sp": to_sp, "tp": to_tp}, device_id_type=MESH_ID)
 
-    blocks = wg_hbm.shape[1] // 128
-    per = mlp_cols // 128
-    first = jnp.minimum(sp * per, blocks - per)
-    cols = pl.ds(pl.multiple_of(first * 128, 128), mlp_cols)
+    cols = pl.ds(pl.multiple_of(core * mlp_cols, 128), mlp_cols)
     loads = [pltpu.make_async_copy(wo_hbm, wo.at[:, pl.ds(0, width)], wsem.at[0]),
              pltpu.make_async_copy(wg_hbm.at[:, cols], wg, wsem.at[1]),
              pltpu.make_async_copy(wu_hbm.at[:, cols], wu, wsem.at[2]),
              pltpu.make_async_copy(wd_hbm.at[cols, :], wd.at[:, pl.ds(0, width)], wsem.at[3])]
-    for cp in loads:
-        cp.start()
+    loads[0].start()
+    pending = []
+
+    def send(copy, *args):
+        copy(*args).start()
+        pending.append(lambda: copy(*args).wait_send())
 
     barrier = pltpu.get_barrier_semaphore()
     for k in range(1, sp_size):
@@ -214,7 +223,7 @@
         return rc(part_ref.at[to], crecv.at[sp], csem.at[0, k - 1], csem.at[1, k - 1], to, tp)
 
     for k in range(1, sp_size):
-        part_copy(k).start()
+        send(part_copy, k)
     pad = CHUNK * tp_size - width
     wo[:, width:] = jnp.zeros((heads_cols, pad), bf)
     wd[:, width:] = jnp.zeros((mlp_cols, pad), bf)
@@ -223,11 +232,14 @@
         toks[:, t, :, :w] = tok_ref[:, t * CHUNK:t * CHUNK + w].astype(f32).reshape(sp_size, group, w)
         if w < CHUNK:
             toks[:, t, :, w:] = jnp.zeros((sp_size, group, CHUNK - w), f32)
+    loads[1].start()
+    loads[2].start()
     crecv[sp] = part_ref[sp]
     for k in range(1, sp_size):
         src = (sp + sp_size - k) % sp_size
         rc(crecv.at[src], crecv.at[src], csem.at[0, k - 1], csem.at[1, k - 1], sp, tp).wait_recv()
 
+    loads[3].start()
     n_rows = part_ref.shape[1] - 8
     n_pairs = n_rows // 8
     span = 128 // (2 * n_pairs)
@@ -260,177 +272,140 @@
         t = (tp + k) % tp_size
         dsend[t] = jnp.dot(attended, wo[:, pl.ds(pl.multiple_of(t * CHUNK, CHUNK), CHUNK)], preferred_element_type=f32)
         if k:
-            proj_copy(k).start()
+            send(proj_copy, k)
     total = toks[sp, tp] + dsend[tp]
     mine = dsend[tp]
     for k in order:
         rc(drecv.at[k - 1], drecv.at[k - 1], dsem.at[0, k - 1], dsem.at[1, k - 1], sp, tp).wait_recv()
         mine = mine + drecv[k - 1]
-    hbuf[sp, tp] = (toks[sp, tp] + mine).astype(bf).astype(f32)
-
-    def gather(buf, which):
-        def chunk(s, t):
-            return buf.at[s, t]
-
-        def own_chunk(d_sp, d_tp, c, k, j):
-            s = (d_sp + sp_size - CORES * (k * (1 - c) + j * c)) % sp_size
-            t = (d_tp + tp_size - (k * c + j * (1 - c))) % tp_size
-            return s, t
-
-        def first_copy(k):
-            return rc(chunk(sp, tp), chunk(sp, tp), asem.at[which, 0, k - 1], asem.at[which, 1, k - 1],
-                      (sp + CORES * k * core) % sp_size, (tp + k * flip) % tp_size)
-
-        def second_copy(k, j):
-            s, t = own_chunk(sp, tp, core, 0, j)
-            return rc(chunk(s, t), chunk(s, t), bsem.at[which, 0, k - 1, j], bsem.at[which, 1, k - 1, j],
-                      (sp + CORES * k * flip) % sp_size, (tp + k * core) % tp_size)
-
-        partner = sp + 1 - 2 * core
-
-        def pair_copy(k, j):
-            s, t = own_chunk(sp, tp, core, k, j)
-            return rc(chunk(s, t), chunk(s, t), psem.at[which, 0, k, j], psem.at[which, 1, k, j], partner, tp)
-
-        for k in order:
-            first_copy(k).start()
-        for k in order:
-            second_copy(k, 0).start()
-        pair_copy(0, 0).start()
-        for j in order:
-            s, t = own_chunk(sp, tp, core, 0, j)
-            rc(chunk(s, t), chunk(s, t), asem.at[which, 0, j - 1], asem.at[which, 1, j - 1], sp, tp).wait_recv()
-            for k in order:
-                second_copy(k, j).start()
-            pair_copy(0, j).start()
-        for j in (0,) + order:
-            for k in order:
-                s, t = own_chunk(sp, tp, core, k, j)
-                rc(chunk(s, t), chunk(s, t), bsem.at[which, 0, k - 1, j], bsem.at[which, 1, k - 1, j], sp, tp).wait_recv()
-                pair_copy(k, j).start()
-        for j in (0,) + order:
-            for k in (0,) + order:
-                s, t = own_chunk(partner, tp, flip, k, j)
-                rc(chunk(s, t), chunk(s, t), psem.at[which, 0, k, j], psem.at[which, 1, k, j], sp, tp).wait_recv()
-        for k in order:
-            first_copy(k).wait_send()
-            for j in range(tp_size):
-                second_copy(k, j).wait_send()
-        for k in range(n_x):
-            for j in range(tp_size):
-                pair_copy(k, j).wait_send()
-
-    gather(hbuf, 0)
-
+    hbuf[core, tp] = (toks[sp, tp] + mine).astype(bf).astype(f32)
+
+    partner = sp + 1 - 2 * core
+
+    def h_copy(k):
+        return rc(hbuf.at[core, tp], hbuf.at[core, tp], hsem.at[0, k - 1], hsem.at[1, k - 1], sp, (tp + k) % tp_size)
+
+    def q_copy(k):
+        t = (tp + tp_size - k) % tp_size
+        return rc(hbuf.at[core, t], hbuf.at[core, t], qsem.at[0, k], qsem.at[1, k], partner, tp)
+
+    for k in order:
+        send(h_copy, k)
+    send(q_copy, 0)
+    for k in order:
+        t = (tp + tp_size - k) % tp_size
+        rc(hbuf.at[core, t], hbuf.at[core, t], hsem.at[0, k - 1], hsem.at[1, k - 1], sp, tp).wait_recv()
+        send(q_copy, k)
+    for k in (0,) + order:
+        t = (tp + tp_size - k) % tp_size
+        rc(hbuf.at[flip, t], hbuf.at[flip, t], qsem.at[0, k], qsem.at[1, k], sp, tp).wait_recv()
+
+    chip_rows = CORES * group
     square = None
     for t in range(tp_size):
         w = min(CHUNK, width - t * CHUNK)
-        v = hbuf[:, t].reshape(rows, CHUNK)[:, :w]
+        v = hbuf[:, t].reshape(chip_rows, CHUNK)[:, :w]
         s = jnp.sum(v * v, axis=-1, keepdims=True)
         square = s if square is None else square + s
     inv = lax.rsqrt(square / width + NORM_EPS)
     for t in range(tp_size):
         w = min(CHUNK, width - t * CHUNK)
-        v = hbuf[:, t].reshape(rows, CHUNK)[:, :w]
-        normed[:, t * CHUNK:t * CHUNK + w] = (v * inv * gain_ref[:, t * CHUNK:t * CHUNK + w].astype(f32)).astype(bf)
+        v = hbuf[:, t].reshape(chip_rows, CHUNK)[:, :w]
+        normed[:, t * CHUNK:t * CHUNK + w] = (v * inv * gain_ref[t * CHUNK:t * CHUNK + w].astype(f32).reshape(1, w)).astype(bf)
     loads[1].wait()
     gate = jnp.dot(normed[...], wg[...], preferred_element_type=f32)
     loads[2].wait()
     up = jnp.dot(normed[...], wu[...], preferred_element_type=f32)
-    block = first + lax.broadcasted_iota(jnp.int32, (rows, mlp_cols), 1) // 128
-    hidden_mlp[...] = jnp.where(block >= sp * per, jax.nn.silu(gate) * up, 0.0).astype(bf)
+    hidden_mlp[...] = (jax.nn.silu(gate) * up).astype(bf)
     loads[3].wait()
 
-    partner = sp + 1 - 2 * core
-
-    def half_copy(t):
-        return rc(dpart.at[:, flip, t], precv.at[:, t], psem.at[2, 0, 0, t], psem.at[2, 1, 0, t], partner, tp)
+    def half_copy(i):
+        t = (tp + i) % tp_size
+        return rc(dpart.at[flip, t], precv.at[i], qsem.at[0, tp_size + i], qsem.at[1, tp_size + i], partner, tp)
+
+    def sum_copy(k):
+        return rc(gsum.at[k], grecv.at[k - 1], gsem.at[0, k - 1], gsem.at[1, k - 1], sp, (tp + k) % tp_size)
+
+    def pair_sum(i):
+        t = (tp + i) % tp_size
+        rc(precv.at[i], precv.at[i], qsem.at[0, tp_size + i], qsem.at[1, tp_size + i], sp, tp).wait_recv()
+        gsum[i] = dpart[core, t] + precv[i]
+        if i:
+            send(sum_copy, i)
 
     steps = order + (0,)
-    for i in steps:
+    for n, i in enumerate(steps):
         t = (tp + i) % tp_size
         part = jnp.dot(hidden_mlp[...], wd[:, pl.ds(pl.multiple_of(t * CHUNK, CHUNK), CHUNK)], preferred_element_type=f32)
-        dpart[:, :, t] = part.reshape(n_x, CORES, group, CHUNK)
-        half_copy(t).start()
-
-    def x_copy(k, t):
-        to = (x + k) % n_x
-        return rc(gsum.at[to, t], g1recv.at[k - 1, t], g1sem.at[0, k - 1, t], g1sem.at[1, k - 1, t], CORES * to + core, tp)
-
-    def y_copy(k, j):
-        to = (tp + k) % tp_size
-        return rc(gsum.at[j, to], g1recv.at[k - 1, j], g1sem.at[0, k - 1, j], g1sem.at[1, k - 1, j], sp, to)
-
-    for i in steps:
-        t = (tp + i) % tp_size
-        rc(precv.at[:, t], precv.at[:, t], psem.at[2, 0, 0, t], psem.at[2, 1, 0, t], sp, tp).wait_recv()
-        gsum[:, t] = dpart[:, core, t] + precv[:, t]
-
-        @pl.when(core == 0)
-        def _():
+        dpart[:, t] = part.reshape(CORES, group, CHUNK)
+        send(half_copy, i)
+        if n >= 2:
+            pair_sum(steps[n - 2])
+    pair_sum(steps[-2])
+    pair_sum(steps[-1])
+    acc = gsum[0]
+    for k in order:
+        rc(grecv.at[k - 1], grecv.at[k - 1], gsem.at[0, k - 1], gsem.at[1, k - 1], sp, tp).wait_recv()
+        acc = acc + grecv[k - 1]
+    obuf[sp, tp] = (hbuf[core, tp] + acc).astype(bf).astype(f32)
+
+    def gather(buf):
+        def chunk(s, t):
+            return buf.at[s, t]
+
+        def own_chunk(d_sp, d_tp, c, k, j):
+            s = (d_sp + sp_size - CORES * (k * (1 - c) + j * c)) % sp_size
+            t = (d_tp + tp_size - (k * c + j * (1 - c))) % tp_size
+            return s, t
+
+        def first_copy(k):
+            return rc(chunk(sp, tp), chunk(sp, tp), asem.at[0, k - 1], asem.at[1, k - 1],
+                      (sp + CORES * k * core) % sp_size, (tp + k * flip) % tp_size)
+
+        def second_copy(k, j):
+            s, t = own_chunk(sp, tp, core, 0, j)
+            return rc(chunk(s, t), chunk(s, t), bsem.at[0, k - 1, j], bsem.at[1, k - 1, j],
+                      (sp + CORES * k * flip) % sp_size, (tp + k * core) % tp_size)
+
+        def pair_copy(k, j):
+            s, t = own_chunk(sp, tp, core, k, j)
+            return rc(chunk(s, t), chunk(s, t), psem.at[0, k, j], psem.at[1, k, j], partner, tp)
+
+        for k in order:
+            send(first_copy, k)
+        for k in order:
+            send(second_copy, k, 0)
+        send(pair_copy, 0, 0)
+        for j in order:
+            s, t = own_chunk(sp, tp, core, 0, j)
+            rc(chunk(s, t), chunk(s, t), asem.at[0, j - 1], asem.at[1, j - 1], sp, tp).wait_recv()
             for k in order:
-                x_copy(k, t).start()
-
-        if i:
-            @pl.when(core == 1)
-            def _():
-                for j in range(n_x):
-                    y_copy(i, j).start()
-
-    b_own = tp * flip + x * core
-
-    def b_copy(k):
-        b = (b_own + k) % tp_size
-        return rc(s1.at[b], g2recv.at[k - 1], g2sem.at[0, k - 1], g2sem.at[1, k - 1],
-                  (sp + CORES * k * core) % sp_size, (tp + k * flip) % tp_size)
-
-    for k in steps:
-        b = (b_own + k) % tp_size
-        acc = gsum[x * flip + b * core, b * flip + tp * core]
-        for a in order:
-            rc(g1recv.at[a - 1, b], g1recv.at[a - 1, b], g1sem.at[0, a - 1, b], g1sem.at[1, a - 1, b], sp, tp).wait_recv()
-            acc = acc + g1recv[a - 1, b]
-        s1[b] = acc
-        if k:
-            b_copy(k).start()
-    acc = s1[b_own]
-    for k in order:
-        rc(g2recv.at[k - 1], g2recv.at[k - 1], g2sem.at[0, k - 1], g2sem.at[1, k - 1], sp, tp).wait_recv()
-        acc = acc + g2recv[k - 1]
-    obuf[sp, tp] = (hbuf[sp, tp] + acc).astype(bf).astype(f32)
-
-    gather(obuf, 1)
+                send(second_copy, k, j)
+            send(pair_copy, 0, j)
+        for j in (0,) + order:
+            for k in order:
+                s, t = own_chunk(sp, tp, core, k, j)
+                rc(chunk(s, t), chunk(s, t), bsem.at[0, k - 1, j], bsem.at[1, k - 1, j], sp, tp).wait_recv()
+                send(pair_copy, k, j)
+        for j in (0,) + order:
+            for k in (0,) + order:
+                s, t = own_chunk(partner, tp, flip, k, j)
+                rc(chunk(s, t), chunk(s, t), psem.at[0, k, j], psem.at[1, k, j], sp, tp).wait_recv()
+
+    gather(obuf)
+
     for t in range(tp_size):
         w = min(CHUNK, width - t * CHUNK)
         out_ref[:, t * CHUNK:t * CHUNK + w] = obuf[:, t].reshape(rows, CHUNK)[:, :w].astype(bf)
-
-    for k in range(1, sp_size):
-        part_copy(k).wait_send()
-    for k in order:
-        proj_copy(k).wait_send()
-        b_copy(k).wait_send()
-    for t in range(tp_size):
-        half_copy(t).wait_send()
-
-    @pl.when(core == 0)
-    def _():
-        for k in order:
-            for t in range(tp_size):
-                x_copy(k, t).wait_send()
-
-    @pl.when(core == 1)
-    def _():
-        for k in order:
-            for j in range(n_x):
-                y_copy(k, j).wait_send()
+    for done in pending:
+        done()
 
 
 def finish(sp_size, tp_size, part, tokens, gain, w_o, w_gate, w_up, w_down):
     rows, width = tokens.shape
     group = rows // sp_size
     n_x = sp_size // CORES
-    blocks = w_gate.shape[1] // 128
-    mlp_cols = -(-blocks // sp_size) * 128
+    mlp_cols = w_gate.shape[1] // CORES
     padded = CHUNK * tp_size
     f32, bf = jnp.float32, jnp.bfloat16
     any_spec = pl.BlockSpec(memory_space=pl.ANY)
@@ -447,17 +422,17 @@
             pltpu.VMEM(part.shape, f32), pltpu.VMEM((2, part.shape[1] - 8, head // 2), f32),
             pltpu.VMEM((sp_size, tp_size, group, CHUNK), f32),
             pltpu.VMEM((tp_size, group, CHUNK), f32), pltpu.VMEM((tp_size - 1, group, CHUNK), f32),
+            pltpu.VMEM((CORES, tp_size, group, CHUNK), f32),
+            pltpu.VMEM((CORES * group, width), bf), pltpu.VMEM((CORES * group, mlp_cols), bf),
+            pltpu.VMEM((CORES, tp_size, group, CHUNK), f32), pltpu.VMEM((tp_size, group, CHUNK), f32), pltpu.VMEM((tp_size, group, CHUNK), f32),
+            pltpu.VMEM((tp_size - 1, group, CHUNK), f32),
             pltpu.VMEM((sp_size, tp_size, group, CHUNK), f32),
-            pltpu.VMEM((rows, width), bf), pltpu.VMEM((rows, mlp_cols), bf),
-            pltpu.VMEM((n_x, CORES, tp_size, group, CHUNK), f32), pltpu.VMEM((n_x, tp_size, group, CHUNK), f32), pltpu.VMEM((n_x, tp_size, group, CHUNK), f32),
-            pltpu.VMEM((3, tp_size, group, CHUNK), f32), pltpu.VMEM((tp_size, group, CHUNK), f32), pltpu.VMEM((3, group, CHUNK), f32),
-            pltpu.VMEM((sp_size, tp_size, group, CHUNK), f32),
-            dma((4,)), dma((2, sp_size - 1)), dma((2, tp_size - 1)), dma((2, 2, 3)), dma((2, 2, 3, tp_size)), dma((3, 2, n_x, tp_size)),
-            dma((2, 3, tp_size)), dma((2, 3)),
+            dma((4,)), dma((2, sp_size - 1)), dma((2, tp_size - 1)), dma((2, tp_size - 1)), dma((2, 2 * tp_size)), dma((2, tp_size - 1)),
+            dma((2, 3)), dma((2, 3, tp_size)), dma((2, n_x, tp_size)),
         ],
-        compiler_params=pltpu.CompilerParams(vmem_limit_bytes=56 << 20, collective_id=0, has_side_effects=True),
+        compiler_params=pltpu.CompilerParams(vmem_limit_bytes=62 << 20, collective_id=0, has_side_effects=True),
         name="finish",
-    )(part, tokens, gain[None, :], w_o, w_gate, w_up, w_down)
+    )(part, tokens, gain, w_o, w_gate, w_up, w_down)
 
 
 from jax.sharding import PartitionSpec as P

time: 85.7 us -> 69.3 us (0.81)
  Pallas kernels: 78.9 us -> 66.6 us
  local copies, waits for them, and re-layouts: 5.81 us -> 1.84 us
    pallas_call x1, Pallas kernels: 54.5 us -> 46.8 us  [finish(): pl.pallas_call(functools.partial(finish_kernel, sp_size, tp_size), out_sh...]
    pallas_call x1, Pallas kernels: 24.4 us -> 19.8 us  [attend(): pl.pallas_call(functools.partial(attend_kernel, sp_size), out_shape=(jax....]
    broadcast_in_dim x3 -> x0, local copies, waits for them, and re-layouts: 3.97 us -> none  [the longest x1 1.36 us: attend(): positions[:, None]]
where the time goes in v3:
time: 69.3 us; the launch traced here: 69.1 us
  Pallas kernels  66.6 us (96%)
  local copies, waits for them, and re-layouts  1.84 us (3%)
    pallas_call x1, Pallas kernels, finish(): pl.pallas_call(functools.partial(finish_kernel, sp_size, tp_size), out_sh...  46.8 us
    pallas_call x1, Pallas kernels, attend(): pl.pallas_call(functools.partial(attend_kernel, sp_size), out_shape=(jax....  19.8 us
    unnamed x1, local copies, waits for them, and re-layouts  1.84 us

profile of v3, /device:TPU:97, one launch (start us, length us, event | category | flops | bytes accessed | tf_op | source)
XLA Modules:
  0.0 69.1 jit_solution(16711687087771178422)
XLA Ops:
  0.6 19.8 %attend.1 = (f32[8,40,256]{2,1,0:T(8,128)}, bf16[64,128,2,256]{3,2,1,0:T(2,128)(2,1)}, bf16[64,128,2,256]{3,2,1,0:T(2,128)(2,1)}) custom-call(bf16[64,3840]{1,0:T(8,128)(2,1)} %tok_ref.3, s32[64]{0:T(128)} %pos_ref.1, f32[1,128]{1,0:T(1,128)} %constant.5.freq_ref, bf16[3840]{0:T(1024)(128)(2,1)} %gain_ref.2, bf16[3840,1024]{1,0:T(8,128)(2,1)} %wq_hbm.1, ...), custom_call_target="tpu_custom_call" | custom-call | tf_op jit(solution)/shard_map/attend/pallas_call | solution.py:160
  20.4 46.8 %finish.1 = bf16[64,3840]{1,0:T(8,128)(2,1)} custom-call(f32[8,40,256]{2,1,0:T(8,128)} %get-tuple-element.6.part_ref, bf16[64,3840]{1,0:T(8,128)(2,1)} %tok_ref.3, bf16[3840]{0:T(1024)(128)(2,1)} %gain_ref.3, bf16[1024,3840]{1,0:T(8,128)(2,1)} %wo_hbm.1, bf16[3840,3840]{1,0:T(8,128)(2,1)} %wg_hbm.1, bf16[3840,3840]{1,0:T(8,128)(2,1)} %wu_hbm.1, ...), custom_call_target="tpu_custom_call" | custom-call | tf_op jit(solution)/shard_map/finish/pallas_call | solution.py:415
  67.3 1.8 %copy.18 = bf16[64,3840]{1,0:T(8,128)(2,1)} copy(bf16[64,3840]{1,0:T(8,128)(2,1)} %finish.1) | data formatting | bytes 983040

commit v4 on v3

--- a/solution.py
+++ b/solution.py
@@ -8,12 +8,12 @@
 ROPE_THETA = 10000.0
 GRP = 8
 KSTEP = 768
-EARLY = 2
-
-
-def attend_kernel(sp_size, tok_ref, pos_ref, freq_ref, gain_ref, wq_hbm, wk_hbm, wv_hbm, ck_hbm, cv_hbm,
+AHEAD = 3
+
+
+def attend_kernel(sp_size, tok_hbm, pos_hbm, freq_hbm, gain_hbm, wq_hbm, wk_hbm, wv_hbm, ck_hbm, cv_hbm,
                   part_ref, nk_hbm, nv_hbm,
-                  wq, wk, wv, kbuf, vbuf, acc, normed, qrows, knew, vnew, posrow, wsem, csem, osem):
+                  tok_ref, pos_ref, freq_ref, gain_ref, wq, wk, wv, kbuf, vbuf, acc, normed, qrows, knew, vnew, posrow, isem, wsem, csem, osem):
     rows, width = tok_ref.shape
     slots_local = kbuf.shape[1]
     kv_heads = kbuf.shape[2]
@@ -41,9 +41,15 @@
         return [pltpu.make_async_copy(kbuf.at[sl], nk_hbm.at[sl], osem.at[0, g]),
                 pltpu.make_async_copy(vbuf.at[sl], nv_hbm.at[sl], osem.at[1, g])]
 
-    for c in range(ksteps):
+    inputs = [pltpu.make_async_copy(src, dst, isem.at[i])
+              for i, (src, dst) in enumerate(((tok_hbm, tok_ref), (pos_hbm, pos_ref), (freq_hbm, freq_ref), (gain_hbm, gain_ref)))]
+    for cp in inputs:
+        cp.start()
+    for c in range(AHEAD):
         for cp in wcopies(c):
             cp.start()
+    for cp in inputs:
+        cp.wait()
     wide = tok_ref[...].astype(jnp.float32)
     inv = lax.rsqrt(jnp.mean(wide * wide, axis=-1, keepdims=True) + NORM_EPS)
     normed[...] = (wide * inv * gain_ref[...].astype(jnp.float32).reshape(1, width)).astype(jnp.bfloat16)
@@ -58,12 +64,15 @@
         for cp in wcopies(c):
             cp.wait()
 
-        for at, these in ((ksteps - 2, range(EARLY)), (ksteps - 1, range(EARLY, groups))):
-            @pl.when(c == at)
-            def _():
-                for g in these:
-                    for cp in ccopies(g):
-                        cp.start()
+        @pl.when(c + AHEAD < ksteps)
+        def _():
+            for cp in wcopies(c + AHEAD):
+                cp.start()
+
+        @pl.when(c + AHEAD >= ksteps)
+        def _():
+            for cp in ccopies(c + AHEAD - ksteps):
+                cp.start()
 
         sl = pl.ds(pl.multiple_of(c * KSTEP, KSTEP), KSTEP)
         lhs = normed[:, sl]
@@ -99,6 +108,12 @@
     def _(g):
         for cp in ccopies(g):
             cp.wait()
+
+        @pl.when(g + AHEAD < groups)
+        def _():
+            for cp in ccopies(g + AHEAD):
+                cp.start()
+
         for i in range(GRP):
             b = g * GRP + i
             local = pos_ref[b] % slots - my_first
@@ -153,26 +168,27 @@
     freq = jnp.asarray((np.float32(ROPE_THETA) ** (np.float32(-2.0) * np.arange(head // 2, dtype=np.float32) / np.float32(head))).astype(np.float32))[None, :]
     groups = rows // GRP
     chunk_rows = GRP * heads + 8
-    any_spec = pl.BlockSpec(memory_space=pl.ANY)
+    any_spec = pl.BlockSpec(memory_space=pltpu.HBM)
     vm = pl.BlockSpec(memory_space=pltpu.VMEM)
     qkv_cols = w_q.shape[1] + 2 * w_k.shape[1]
     bf = jnp.bfloat16
     return pl.pallas_call(
         functools.partial(attend_kernel, sp_size),
-        out_shape=(jax.ShapeDtypeStruct((groups, chunk_rows, head), jnp.float32),
+        out_shape=(pltpu.VMEM((groups, chunk_rows, head), jnp.float32),
                    jax.ShapeDtypeStruct(cache_k.shape, bf), jax.ShapeDtypeStruct(cache_v.shape, bf)),
-        in_specs=[vm, pl.BlockSpec(memory_space=pltpu.SMEM), vm, vm] + [any_spec] * 5,
+        in_specs=[any_spec] * 9,
         out_specs=(vm, any_spec, any_spec),
         scratch_shapes=[
+            pltpu.VMEM(tokens.shape, bf), pltpu.SMEM(positions.shape, jnp.int32), pltpu.VMEM((1, head // 2), jnp.float32), pltpu.VMEM(gain.shape, bf),
             pltpu.VMEM(w_q.shape, bf), pltpu.VMEM(w_k.shape, bf), pltpu.VMEM(w_v.shape, bf),
             pltpu.VMEM(cache_k.shape, bf), pltpu.VMEM(cache_v.shape, bf),
             pltpu.VMEM((rows, qkv_cols), jnp.float32), pltpu.VMEM((rows, width), bf),
             pltpu.VMEM((2, rows * heads, head // 2), jnp.float32),
             pltpu.VMEM((rows, kv_heads, head), jnp.float32), pltpu.VMEM((rows, kv_heads, head), jnp.float32),
             pltpu.VMEM((rows, head // 2), jnp.int32),
-            pltpu.SemaphoreType.DMA((3, width // KSTEP)), pltpu.SemaphoreType.DMA((2, groups)), pltpu.SemaphoreType.DMA((2, groups)),
+            pltpu.SemaphoreType.DMA((4,)), pltpu.SemaphoreType.DMA((3, width // KSTEP)), pltpu.SemaphoreType.DMA((2, groups)), pltpu.SemaphoreType.DMA((2, groups)),
         ],
-        compiler_params=pltpu.CompilerParams(vmem_limit_bytes=56 << 20),
+        compiler_params=pltpu.CompilerParams(vmem_limit_bytes=66_000_000),
         name="attend",
     )(tokens, positions, freq, gain, w_q, w_k, w_v, cache_k, cache_v)
 
@@ -182,8 +198,8 @@
 CORES = 2
 
 
-def finish_kernel(sp_size, tp_size, part_ref, tok_ref, gain_ref, wo_hbm, wg_hbm, wu_hbm, wd_hbm, out_ref,
-                  wo, wg, wu, wd, crecv, att, toks, dsend, drecv, hbuf, normed, hidden_mlp, dpart, precv, gsum, grecv, obuf,
+def finish_kernel(sp_size, tp_size, part_ref, tok_hbm, gain_hbm, wo_hbm, wg_hbm, wu_hbm, wd_hbm, out_ref,
+                  tok_ref, gain_ref, wo, wg, wu, wd, crecv, att, toks, dsend, drecv, hbuf, normed, hidden_mlp, dpart, precv, gsum, grecv, obuf,
                   wsem, csem, dsem, hsem, qsem, gsem, asem, bsem, psem):
     f32, bf = jnp.float32, jnp.bfloat16
     rows, width = tok_ref.shape
@@ -203,8 +219,11 @@
     loads = [pltpu.make_async_copy(wo_hbm, wo.at[:, pl.ds(0, width)], wsem.at[0]),
              pltpu.make_async_copy(wg_hbm.at[:, cols], wg, wsem.at[1]),
              pltpu.make_async_copy(wu_hbm.at[:, cols], wu, wsem.at[2]),
-             pltpu.make_async_copy(wd_hbm.at[cols, :], wd.at[:, pl.ds(0, width)], wsem.at[3])]
-    loads[0].start()
+             pltpu.make_async_copy(wd_hbm.at[cols, :], wd.at[:, pl.ds(0, width)], wsem.at[3]),
+             pltpu.make_async_copy(tok_hbm, tok_ref, wsem.at[4]),
+             pltpu.make_async_copy(gain_hbm, gain_ref, wsem.at[5])]
+    for cp in (loads[4], loads[5], loads[0]):
+        cp.start()
     pending = []
 
     def send(copy, *args):
@@ -222,24 +241,25 @@
         to = (sp + k) % sp_size
         return rc(part_ref.at[to], crecv.at[sp], csem.at[0, k - 1], csem.at[1, k - 1], to, tp)
 
-    for k in range(1, sp_size):
+    for k in sorted(range(1, sp_size), key=lambda k: abs(k - sp_size // 2)):
         send(part_copy, k)
     pad = CHUNK * tp_size - width
     wo[:, width:] = jnp.zeros((heads_cols, pad), bf)
     wd[:, width:] = jnp.zeros((mlp_cols, pad), bf)
+    loads[4].wait()
+    loads[5].wait()
     for t in range(tp_size):
         w = min(CHUNK, width - t * CHUNK)
         toks[:, t, :, :w] = tok_ref[:, t * CHUNK:t * CHUNK + w].astype(f32).reshape(sp_size, group, w)
         if w < CHUNK:
             toks[:, t, :, w:] = jnp.zeros((sp_size, group, CHUNK - w), f32)
     loads[1].start()
-    loads[2].start()
     crecv[sp] = part_ref[sp]
     for k in range(1, sp_size):
         src = (sp + sp_size - k) % sp_size
         rc(crecv.at[src], crecv.at[src], csem.at[0, k - 1], csem.at[1, k - 1], sp, tp).wait_recv()
 
-    loads[3].start()
+    loads[2].start()
     n_rows = part_ref.shape[1] - 8
     n_pairs = n_rows // 8
     span = 128 // (2 * n_pairs)
@@ -267,8 +287,8 @@
         to = (tp + k) % tp_size
         return rc(dsend.at[to], drecv.at[k - 1], dsem.at[0, k - 1], dsem.at[1, k - 1], sp, to)
 
-    order = (1, 3, 2) if tp_size == 4 else tuple(range(1, tp_size))
-    for k in order + (0,):
+    far_first, order = (2, 1, 3), (1, 3, 2)
+    for k in far_first + (0,):
         t = (tp + k) % tp_size
         dsend[t] = jnp.dot(attended, wo[:, pl.ds(pl.multiple_of(t * CHUNK, CHUNK), CHUNK)], preferred_element_type=f32)
         if k:
@@ -280,6 +300,8 @@
         mine = mine + drecv[k - 1]
     hbuf[core, tp] = (toks[sp, tp] + mine).astype(bf).astype(f32)
 
+    loads[3].start()
+
     partner = sp + 1 - 2 * core
 
     def h_copy(k):
@@ -289,7 +311,7 @@
         t = (tp + tp_size - k) % tp_size
         return rc(hbuf.at[core, t], hbuf.at[core, t], qsem.at[0, k], qsem.at[1, k], partner, tp)
 
-    for k in order:
+    for k in far_first:
         send(h_copy, k)
     send(q_copy, 0)
     for k in order:
@@ -333,7 +355,7 @@
         if i:
             send(sum_copy, i)
 
-    steps = order + (0,)
+    steps = far_first + (0,)
     for n, i in enumerate(steps):
         t = (tp + i) % tp_size
         part = jnp.dot(hidden_mlp[...], wd[:, pl.ds(pl.multiple_of(t * CHUNK, CHUNK), CHUNK)], preferred_element_type=f32)
@@ -371,15 +393,15 @@
             s, t = own_chunk(sp, tp, core, k, j)
             return rc(chunk(s, t), chunk(s, t), psem.at[0, k, j], psem.at[1, k, j], partner, tp)
 
-        for k in order:
+        for k in far_first:
             send(first_copy, k)
-        for k in order:
+        for k in far_first:
             send(second_copy, k, 0)
         send(pair_copy, 0, 0)
         for j in order:
             s, t = own_chunk(sp, tp, core, 0, j)
             rc(chunk(s, t), chunk(s, t), asem.at[0, j - 1], asem.at[1, j - 1], sp, tp).wait_recv()
-            for k in order:
+            for k in far_first:
                 send(second_copy, k, j)
             send(pair_copy, 0, j)
         for j in (0,) + order:
@@ -408,16 +430,17 @@
     mlp_cols = w_gate.shape[1] // CORES
     padded = CHUNK * tp_size
     f32, bf = jnp.float32, jnp.bfloat16
-    any_spec = pl.BlockSpec(memory_space=pl.ANY)
+    any_spec = pl.BlockSpec(memory_space=pltpu.HBM)
     vm = pl.BlockSpec(memory_space=pltpu.VMEM)
     dma = pltpu.SemaphoreType.DMA
     head = part.shape[2]
     return pl.pallas_call(
         functools.partial(finish_kernel, sp_size, tp_size),
-        out_shape=jax.ShapeDtypeStruct((rows, width), bf),
-        in_specs=[vm, vm, vm] + [any_spec] * 4,
+        out_shape=pltpu.VMEM((rows, width), bf),
+        in_specs=[vm] + [any_spec] * 6,
         out_specs=vm,
         scratch_shapes=[
+            pltpu.VMEM(tokens.shape, bf), pltpu.VMEM(gain.shape, bf),
             pltpu.VMEM((w_o.shape[0], padded), bf), pltpu.VMEM((width, mlp_cols), bf), pltpu.VMEM((width, mlp_cols), bf), pltpu.VMEM((mlp_cols, padded), bf),
             pltpu.VMEM(part.shape, f32), pltpu.VMEM((2, part.shape[1] - 8, head // 2), f32),
             pltpu.VMEM((sp_size, tp_size, group, CHUNK), f32),
@@ -427,10 +450,10 @@
             pltpu.VMEM((CORES, tp_size, group, CHUNK), f32), pltpu.VMEM((tp_size, group, CHUNK), f32), pltpu.VMEM((tp_size, group, CHUNK), f32),
             pltpu.VMEM((tp_size - 1, group, CHUNK), f32),
             pltpu.VMEM((sp_size, tp_size, group, CHUNK), f32),
-            dma((4,)), dma((2, sp_size - 1)), dma((2, tp_size - 1)), dma((2, tp_size - 1)), dma((2, 2 * tp_size)), dma((2, tp_size - 1)),
+            dma((6,)), dma((2, sp_size - 1)), dma((2, tp_size - 1)), dma((2, tp_size - 1)), dma((2, 2 * tp_size)), dma((2, tp_size - 1)),
             dma((2, 3)), dma((2, 3, tp_size)), dma((2, n_x, tp_size)),
         ],
-        compiler_params=pltpu.CompilerParams(vmem_limit_bytes=62 << 20, collective_id=0, has_side_effects=True),
+        compiler_params=pltpu.CompilerParams(vmem_limit_bytes=65_500_000, collective_id=0, has_side_effects=True),
         name="finish",
     )(part, tokens, gain, w_o, w_gate, w_up, w_down)
 
@@ -448,6 +471,7 @@
 
     def local_step(tokens, positions, cache_k, cache_v, attn_gain, w_q, w_k, w_v, w_o, mlp_gain, w_gate, w_up, w_down):
         part, new_k, new_v = attend(sp_size, tokens, positions, cache_k, cache_v, attn_gain, w_q, w_k, w_v)
+        part = pltpu.with_memory_space_constraint(part, pltpu.VMEM)
         layer_out = finish(sp_size, tp_size, part, tokens, mlp_gain, w_o, w_gate, w_up, w_down)
         return layer_out, new_k, new_v
 

time: 69.3 us -> 65.7 us (0.948)
  Pallas kernels: 66.6 us -> 64.1 us
  local copies, waits for them, and re-layouts: 1.84 us -> 0.78 us
    pallas_call x1, Pallas kernels: 46.8 us -> 44.3 us  [finish(): pl.pallas_call(functools.partial(finish_kernel, sp_size, tp_size), out_sh...]
    unnamed x1, local copies, waits for them, and re-layouts: 1.84 us -> 0.78 us
where the time goes in v4:
time: 65.7 us; the launch traced here: 65.5 us
  Pallas kernels  64.1 us (98%)
  local copies, waits for them, and re-layouts  0.78 us (1%)
    pallas_call x1, Pallas kernels, finish(): pl.pallas_call(functools.partial(finish_kernel, sp_size, tp_size), out_sh...  44.3 us
    pallas_call x1, Pallas kernels, attend(): pl.pallas_call(functools.partial(attend_kernel, sp_size), out_shape=(pltp...  19.8 us

profile of v4, /device:TPU:97, one launch (start us, length us, event | category | flops | bytes accessed | tf_op | source)
XLA Modules:
  0.0 65.5 jit_solution(17862474426272915291)
XLA Ops:
  0.6 19.8 %attend.1 = (f32[8,40,256]{2,1,0:T(8,128)S(1)}, bf16[64,128,2,256]{3,2,1,0:T(2,128)(2,1)}, bf16[64,128,2,256]{3,2,1,0:T(2,128)(2,1)}) custom-call(bf16[64,3840]{1,0:T(8,128)(2,1)} %tok_hbm.3, s32[64]{0:T(128)} %pos_hbm.1, f32[1,128]{1,0:T(1,128)} %constant.5.freq_hbm, bf16[3840]{0:T(1024)(128)(2,1)} %gain_hbm.2, bf16[3840,1024]{1,0:T(8,128)(2,1)} %wq_hbm.1, ...), custom_call_target="tpu_custom_call" | custom-call | tf_op jit(solution)/shard_map/attend/pallas_call | solution.py:175
  20.5 44.3 %finish.1 = bf16[64,3840]{1,0:T(8,128)(2,1)S(1)} custom-call(f32[8,40,256]{2,1,0:T(8,128)S(1)} %get-tuple-element.6.part_ref, bf16[64,3840]{1,0:T(8,128)(2,1)} %tok_hbm.3, bf16[3840]{0:T(1024)(128)(2,1)} %gain_hbm.3, bf16[1024,3840]{1,0:T(8,128)(2,1)} %wo_hbm.1, bf16[3840,3840]{1,0:T(8,128)(2,1)} %wg_hbm.1, bf16[3840,3840]{1,0:T(8,128)(2,1)} %wu_hbm.1, ...), custom_call_target="tpu_custom_call" | custom-call | tf_op jit(solution)/shard_map/finish/pallas_call | solution.py:437
  64.7 0.8 %copy.18 = bf16[64,3840]{1,0:T(8,128)(2,1)} copy(bf16[64,3840]{1,0:T(8,128)(2,1)S(1)} %finish.1) | data formatting | bytes 983040

commit v5 on v4

--- a/solution.py
+++ b/solution.py
@@ -117,11 +117,10 @@
         for i in range(GRP):
             b = g * GRP + i
             local = pos_ref[b] % slots - my_first
-
-            @pl.when((local >= 0) & (local < slots_local))
-            def _():
-                kbuf[b, local] = knew[b].astype(jnp.bfloat16)
-                vbuf[b, local] = vnew[b].astype(jnp.bfloat16)
+            here = (local >= 0) & (local < slots_local)
+            at = jnp.clip(local, 0, slots_local - 1)
+            for buf, new in ((kbuf, knew), (vbuf, vnew)):
+                buf[b, at] = jnp.where(here, new[b], buf[b, at].astype(jnp.float32)).astype(jnp.bfloat16)
         for cp in ocopies(g):
             cp.start()
         stat = jnp.zeros((8, 128), jnp.float32)
@@ -195,14 +194,15 @@
 
 MESH_ID = pl.DeviceIdType.MESH
 CHUNK = 1024
+SUB = 512
 CORES = 2
 
 
 def finish_kernel(sp_size, tp_size, part_ref, tok_hbm, gain_hbm, wo_hbm, wg_hbm, wu_hbm, wd_hbm, out_ref,
-                  tok_ref, gain_ref, wo, wg, wu, wd, crecv, att, toks, dsend, drecv, hbuf, normed, hidden_mlp, dpart, precv, gsum, grecv, obuf,
+                  tok_ref, gain_ref, wo, wg, wu, wd, crecv, att, dsend, drecv, hbuf, hflat, normed, ubuf, gsum, grecv, obuf,
                   wsem, csem, dsem, hsem, qsem, gsem, asem, bsem, psem):
     f32, bf = jnp.float32, jnp.bfloat16
-    rows, width = tok_ref.shape
+    rows, width = tok_hbm.shape
     n_x = sp_size // CORES
     heads_cols = wo.shape[0]
     mlp_cols = wg.shape[1]
@@ -216,14 +216,28 @@
                                             device_id={"sp": to_sp, "tp": to_tp}, device_id_type=MESH_ID)
 
     cols = pl.ds(pl.multiple_of(core * mlp_cols, 128), mlp_cols)
+    half_width = width // CORES
+    out_cols = pl.ds(pl.multiple_of(core * half_width, 128), half_width)
     loads = [pltpu.make_async_copy(wo_hbm, wo.at[:, pl.ds(0, width)], wsem.at[0]),
              pltpu.make_async_copy(wg_hbm.at[:, cols], wg, wsem.at[1]),
              pltpu.make_async_copy(wu_hbm.at[:, cols], wu, wsem.at[2]),
-             pltpu.make_async_copy(wd_hbm.at[cols, :], wd.at[:, pl.ds(0, width)], wsem.at[3]),
-             pltpu.make_async_copy(tok_hbm, tok_ref, wsem.at[4]),
-             pltpu.make_async_copy(gain_hbm, gain_ref, wsem.at[5])]
-    for cp in (loads[4], loads[5], loads[0]):
-        cp.start()
+             pltpu.make_async_copy(wd_hbm.at[cols, out_cols], wd.at[0, :, pl.ds(0, half_width)], wsem.at[3]),
+             pltpu.make_async_copy(gain_hbm, gain_ref, wsem.at[4]),
+             pltpu.make_async_copy(wd_hbm.at[pl.ds(pl.multiple_of(flip * mlp_cols, 128), mlp_cols), out_cols], wd.at[1, :, pl.ds(0, half_width)], wsem.at[6])]
+    whole, rest = divmod(width, CHUNK)
+
+    def tokens_chunk(act):
+        def run(w):
+            src = tok_hbm.at[pl.ds(pl.multiple_of(sp * group, group), group), pl.ds(pl.multiple_of(tp * CHUNK, CHUNK), w)]
+            act(pltpu.make_async_copy(src, tok_ref.at[:, pl.ds(0, w)], wsem.at[5]))
+
+        pl.when(tp < whole)(lambda: run(CHUNK))
+        if rest:
+            pl.when(tp == whole)(lambda: run(rest))
+
+    tokens_chunk(lambda cp: cp.start())
+    loads[4].start()
+    loads[0].start()
     pending = []
 
     def send(copy, *args):
@@ -245,14 +259,13 @@
         send(part_copy, k)
     pad = CHUNK * tp_size - width
     wo[:, width:] = jnp.zeros((heads_cols, pad), bf)
-    wd[:, width:] = jnp.zeros((mlp_cols, pad), bf)
+    wd[:, :, half_width:] = jnp.zeros((CORES, mlp_cols, SUB * tp_size - half_width), bf)
+    if rest:
+        @pl.when(tp == whole)
+        def _():
+            tok_ref[:, rest:] = jnp.zeros((group, CHUNK - rest), bf)
     loads[4].wait()
-    loads[5].wait()
-    for t in range(tp_size):
-        w = min(CHUNK, width - t * CHUNK)
-        toks[:, t, :, :w] = tok_ref[:, t * CHUNK:t * CHUNK + w].astype(f32).reshape(sp_size, group, w)
-        if w < CHUNK:
-            toks[:, t, :, w:] = jnp.zeros((sp_size, group, CHUNK - w), f32)
+    tokens_chunk(lambda cp: cp.wait())
     loads[1].start()
     crecv[sp] = part_ref[sp]
     for k in range(1, sp_size):
@@ -293,14 +306,14 @@
         dsend[t] = jnp.dot(attended, wo[:, pl.ds(pl.multiple_of(t * CHUNK, CHUNK), CHUNK)], preferred_element_type=f32)
         if k:
             send(proj_copy, k)
-    total = toks[sp, tp] + dsend[tp]
     mine = dsend[tp]
     for k in order:
         rc(drecv.at[k - 1], drecv.at[k - 1], dsem.at[0, k - 1], dsem.at[1, k - 1], sp, tp).wait_recv()
         mine = mine + drecv[k - 1]
-    hbuf[core, tp] = (toks[sp, tp] + mine).astype(bf).astype(f32)
+    hbuf[core, tp] = (tok_ref[...].astype(f32) + mine).astype(bf).astype(f32)
 
     loads[3].start()
+    loads[5].start()
 
     partner = sp + 1 - 2 * core
 
@@ -327,6 +340,7 @@
     for t in range(tp_size):
         w = min(CHUNK, width - t * CHUNK)
         v = hbuf[:, t].reshape(chip_rows, CHUNK)[:, :w]
+        hflat[:, t * CHUNK:t * CHUNK + w] = v
         s = jnp.sum(v * v, axis=-1, keepdims=True)
         square = s if square is None else square + s
     inv = lax.rsqrt(square / width + NORM_EPS)
@@ -338,42 +352,38 @@
     gate = jnp.dot(normed[...], wg[...], preferred_element_type=f32)
     loads[2].wait()
     up = jnp.dot(normed[...], wu[...], preferred_element_type=f32)
-    hidden_mlp[...] = (jax.nn.silu(gate) * up).astype(bf)
-    loads[3].wait()
-
-    def half_copy(i):
-        t = (tp + i) % tp_size
-        return rc(dpart.at[flip, t], precv.at[i], qsem.at[0, tp_size + i], qsem.at[1, tp_size + i], partner, tp)
+    hflat[:, width:] = jnp.zeros((chip_rows, CHUNK * tp_size - width), f32)
+    ubuf[core] = (jax.nn.silu(gate) * up).astype(bf).astype(f32)
+
+    def u_copy():
+        return rc(ubuf.at[core], ubuf.at[core], qsem.at[0, tp_size], qsem.at[1, tp_size], partner, tp)
 
     def sum_copy(k):
         return rc(gsum.at[k], grecv.at[k - 1], gsem.at[0, k - 1], gsem.at[1, k - 1], sp, (tp + k) % tp_size)
 
-    def pair_sum(i):
-        t = (tp + i) % tp_size
-        rc(precv.at[i], precv.at[i], qsem.at[0, tp_size + i], qsem.at[1, tp_size + i], sp, tp).wait_recv()
-        gsum[i] = dpart[core, t] + precv[i]
-        if i:
-            send(sum_copy, i)
-
+    send(u_copy)
     steps = far_first + (0,)
-    for n, i in enumerate(steps):
-        t = (tp + i) % tp_size
-        part = jnp.dot(hidden_mlp[...], wd[:, pl.ds(pl.multiple_of(t * CHUNK, CHUNK), CHUNK)], preferred_element_type=f32)
-        dpart[:, t] = part.reshape(CORES, group, CHUNK)
-        send(half_copy, i)
-        if n >= 2:
-            pair_sum(steps[n - 2])
-    pair_sum(steps[-2])
-    pair_sum(steps[-1])
+    for half in range(CORES):
+        if half:
+            rc(ubuf.at[flip], ubuf.at[flip], qsem.at[0, tp_size], qsem.at[1, tp_size], sp, tp).wait_recv()
+        u = (ubuf[flip] if half else ubuf[core]).astype(bf)
+        loads[5 if half else 3].wait()
+        for i in steps:
+            at = pl.ds(pl.multiple_of((tp + i) % tp_size * SUB, SUB), SUB)
+            part = jnp.dot(u, wd[half, :, at], preferred_element_type=f32)
+            gsum[i] = gsum[i] + part if half else part
+            if half and i:
+                send(sum_copy, i)
     acc = gsum[0]
     for k in order:
         rc(grecv.at[k - 1], grecv.at[k - 1], gsem.at[0, k - 1], gsem.at[1, k - 1], sp, tp).wait_recv()
         acc = acc + grecv[k - 1]
-    obuf[sp, tp] = (hbuf[core, tp] + acc).astype(bf).astype(f32)
+    mine = pl.ds(pl.multiple_of(core * half_width + tp * SUB, 128), SUB)
+    obuf[x, core, tp] = (hflat[:, mine] + acc).astype(bf).astype(f32)
 
     def gather(buf):
         def chunk(s, t):
-            return buf.at[s, t]
+            return buf.at[s // CORES, s % CORES, t]
 
         def own_chunk(d_sp, d_tp, c, k, j):
             s = (d_sp + sp_size - CORES * (k * (1 - c) + j * c)) % sp_size
@@ -416,9 +426,11 @@
 
     gather(obuf)
 
-    for t in range(tp_size):
-        w = min(CHUNK, width - t * CHUNK)
-        out_ref[:, t * CHUNK:t * CHUNK + w] = obuf[:, t].reshape(rows, CHUNK)[:, :w].astype(bf)
+    for c in range(CORES):
+        for t in range(tp_size):
+            w = min(SUB, half_width - t * SUB)
+            lo = c * half_width + t * SUB
+            out_ref[:, lo:lo + w] = obuf[:, c, t].reshape(rows, SUB)[:, :w].astype(bf)
     for done in pending:
         done()
 
@@ -440,17 +452,15 @@
         in_specs=[vm] + [any_spec] * 6,
         out_specs=vm,
         scratch_shapes=[
-            pltpu.VMEM(tokens.shape, bf), pltpu.VMEM(gain.shape, bf),
-            pltpu.VMEM((w_o.shape[0], padded), bf), pltpu.VMEM((width, mlp_cols), bf), pltpu.VMEM((width, mlp_cols), bf), pltpu.VMEM((mlp_cols, padded), bf),
+            pltpu.VMEM((group, CHUNK), bf), pltpu.VMEM(gain.shape, bf),
+            pltpu.VMEM((w_o.shape[0], padded), bf), pltpu.VMEM((width, mlp_cols), bf), pltpu.VMEM((width, mlp_cols), bf), pltpu.VMEM((CORES, mlp_cols, SUB * tp_size), bf),
             pltpu.VMEM(part.shape, f32), pltpu.VMEM((2, part.shape[1] - 8, head // 2), f32),
-            pltpu.VMEM((sp_size, tp_size, group, CHUNK), f32),
             pltpu.VMEM((tp_size, group, CHUNK), f32), pltpu.VMEM((tp_size - 1, group, CHUNK), f32),
             pltpu.VMEM((CORES, tp_size, group, CHUNK), f32),
-            pltpu.VMEM((CORES * group, width), bf), pltpu.VMEM((CORES * group, mlp_cols), bf),
-            pltpu.VMEM((CORES, tp_size, group, CHUNK), f32), pltpu.VMEM((tp_size, group, CHUNK), f32), pltpu.VMEM((tp_size, group, CHUNK), f32),
-            pltpu.VMEM((tp_size - 1, group, CHUNK), f32),
-            pltpu.VMEM((sp_size, tp_size, group, CHUNK), f32),
-            dma((6,)), dma((2, sp_size - 1)), dma((2, tp_size - 1)), dma((2, tp_size - 1)), dma((2, 2 * tp_size)), dma((2, tp_size - 1)),
+            pltpu.VMEM((CORES * group, padded), f32), pltpu.VMEM((CORES * group, width), bf), pltpu.VMEM((CORES, CORES * group, mlp_cols), f32),
+            pltpu.VMEM((tp_size, CORES * group, SUB), f32), pltpu.VMEM((tp_size - 1, CORES * group, SUB), f32),
+            pltpu.VMEM((n_x, CORES, tp_size, CORES * group, SUB), f32),
+            dma((7,)), dma((2, sp_size - 1)), dma((2, tp_size - 1)), dma((2, tp_size - 1)), dma((2, tp_size + 1)), dma((2, tp_size - 1)),
             dma((2, 3)), dma((2, 3, tp_size)), dma((2, n_x, tp_size)),
         ],
         compiler_params=pltpu.CompilerParams(vmem_limit_bytes=65_500_000, collective_id=0, has_side_effects=True),

time: 65.7 us -> 64.8 us (0.986)
  Pallas kernels: 64.1 us -> 63.3 us
where the time goes in v5:
time: 64.8 us
  Pallas kernels  63.3 us (98%)
  local copies, waits for them, and re-layouts  0.78 us (1%)
  between operations  0.65 us (1%)
    pallas_call x1, Pallas kernels, finish(): pl.pallas_call(functools.partial(finish_kernel, sp_size, tp_size), out_sh...  43.7 us
    pallas_call x1, Pallas kernels, attend(): pl.pallas_call(functools.partial(attend_kernel, sp_size), out_shape=(pltp...  19.6 us

profile of v5, /device:TPU:97, one launch (start us, length us, event | category | flops | bytes accessed | tf_op | source)
XLA Modules:
  0.0 64.8 jit_solution(18295094025181718370)
XLA Ops:
  0.6 19.6 %attend.1 = (f32[8,40,256]{2,1,0:T(8,128)S(1)}, bf16[64,128,2,256]{3,2,1,0:T(2,128)(2,1)}, bf16[64,128,2,256]{3,2,1,0:T(2,128)(2,1)}) custom-call(bf16[64,3840]{1,0:T(8,128)(2,1)} %tok_hbm.3, s32[64]{0:T(128)} %pos_hbm.1, f32[1,128]{1,0:T(1,128)} %constant.5.freq_hbm, bf16[3840]{0:T(1024)(128)(2,1)} %gain_hbm.2, bf16[3840,1024]{1,0:T(8,128)(2,1)} %wq_hbm.1, ...), custom_call_target="tpu_custom_call" | custom-call | tf_op jit(solution)/shard_map/attend/pallas_call | solution.py:174
  20.3 43.7 %finish.1 = bf16[64,3840]{1,0:T(8,128)(2,1)S(1)} custom-call(f32[8,40,256]{2,1,0:T(8,128)S(1)} %get-tuple-element.6.part_ref, bf16[64,3840]{1,0:T(8,128)(2,1)} %tok_hbm.3, bf16[3840]{0:T(1024)(128)(2,1)} %gain_hbm.3, bf16[1024,3840]{1,0:T(8,128)(2,1)} %wo_hbm.1, bf16[3840,3840]{1,0:T(8,128)(2,1)} %wg_hbm.1, bf16[3840,3840]{1,0:T(8,128)(2,1)} %wu_hbm.1, ...), custom_call_target="tpu_custom_call" | custom-call | tf_op jit(solution)/shard_map/finish/pallas_call | solution.py:449
  64.0 0.8 %copy.18 = bf16[64,3840]{1,0:T(8,128)(2,1)} copy(bf16[64,3840]{1,0:T(8,128)(2,1)S(1)} %finish.1) | data formatting | bytes 983040

commit v6 on v5

--- a/solution.py
+++ b/solution.py
@@ -414,8 +414,9 @@
             for k in far_first:
                 send(second_copy, k, j)
             send(pair_copy, 0, j)
-        for j in (0,) + order:
-            for k in order:
+        arrivals = sorted(((k, j) for k in order for j in (0,) + order), key=lambda kj: ((kj[0] == 2) + (0, 2, 3, 2)[kj[1]], kj))
+        for k, j in arrivals:
+            if k:
                 s, t = own_chunk(sp, tp, core, k, j)
                 rc(chunk(s, t), chunk(s, t), bsem.at[0, k - 1, j], bsem.at[1, k - 1, j], sp, tp).wait_recv()
                 send(pair_copy, k, j)

time: 64.8 us -> 64.9 us (level)
  no operation moved by 1% of the time
where the time goes in v6:
time: 64.9 us; the launch traced here: 64.8 us
  Pallas kernels  63.4 us (98%)
  local copies, waits for them, and re-layouts  0.78 us (1%)
  between operations  0.65 us (1%)
    pallas_call x1, Pallas kernels, finish(): pl.pallas_call(functools.partial(finish_kernel, sp_size, tp_size), out_sh...  43.8 us
    pallas_call x1, Pallas kernels, attend(): pl.pallas_call(functools.partial(attend_kernel, sp_size), out_shape=(pltp...  19.6 us

profile of v6, /device:TPU:97, one launch (start us, length us, event | category | flops | bytes accessed | tf_op | source)
XLA Modules:
  0.0 64.8 jit_solution(16905365994574236062)
XLA Ops:
  0.6 19.6 %attend.1 = (f32[8,40,256]{2,1,0:T(8,128)S(1)}, bf16[64,128,2,256]{3,2,1,0:T(2,128)(2,1)}, bf16[64,128,2,256]{3,2,1,0:T(2,128)(2,1)}) custom-call(bf16[64,3840]{1,0:T(8,128)(2,1)} %tok_hbm.3, s32[64]{0:T(128)} %pos_hbm.1, f32[1,128]{1,0:T(1,128)} %constant.5.freq_hbm, bf16[3840]{0:T(1024)(128)(2,1)} %gain_hbm.2, bf16[3840,1024]{1,0:T(8,128)(2,1)} %wq_hbm.1, ...), custom_call_target="tpu_custom_call" | custom-call | tf_op jit(solution)/shard_map/attend/pallas_call | solution.py:174
  20.3 43.8 %finish.1 = bf16[64,3840]{1,0:T(8,128)(2,1)S(1)} custom-call(f32[8,40,256]{2,1,0:T(8,128)S(1)} %get-tuple-element.6.part_ref, bf16[64,3840]{1,0:T(8,128)(2,1)} %tok_hbm.3, bf16[3840]{0:T(1024)(128)(2,1)} %gain_hbm.3, bf16[1024,3840]{1,0:T(8,128)(2,1)} %wo_hbm.1, bf16[3840,3840]{1,0:T(8,128)(2,1)} %wg_hbm.1, bf16[3840,3840]{1,0:T(8,128)(2,1)} %wu_hbm.1, ...), custom_call_target="tpu_custom_call" | custom-call | tf_op jit(solution)/shard_map/finish/pallas_call | solution.py:450
  64.1 0.8 %copy.18 = bf16[64,3840]{1,0:T(8,128)(2,1)} copy(bf16[64,3840]{1,0:T(8,128)(2,1)S(1)} %finish.1) | data formatting | bytes 983040
